TPU v7x, 32 devices: a whole 2x2x4 slice. The times are simulated.
32 devices in a mesh: rep: 4 (over y, x), fsdp: 4 (over z), seq: 2 (over core).
Axes of the slice: x: 2, y: 2, z: 4, core: 2. Of those that a mesh axis runs over, the one named last changes fastest.
Arguments:
- layer_input: bfloat16 [2, 16, 1024, 768], P(None, ('rep', 'fsdp'), 'seq'), may hold values from -6 to 6
- segment: int32 [2, 16, 1024], P(None, ('rep', 'fsdp')), may hold values from 0 to 3, never falling along the last dimension, each value on 1 to 512 neighbouring positions
- rand_blocks: int32 [2, 16, 12, 16, 3], P(None, ('rep', 'fsdp')), may hold values from 0 to 15
- first_gain: bfloat16 [768], P('fsdp'), may hold values from 0.099609375 to 1.8984375
- first_bias: bfloat16 [768], P('fsdp'), may hold values from -1.75 to 1.75
- query_weight: bfloat16 [768, 768], P('fsdp'), may hold values from -0.21875 to 0.21875
- query_bias: bfloat16 [768], P('fsdp'), may hold values from -1.75 to 1.75
- key_weight: bfloat16 [768, 768], P('fsdp'), may hold values from -0.21875 to 0.21875
- value_weight: bfloat16 [768, 768], P('fsdp'), may hold values from -0.21875 to 0.21875
- value_bias: bfloat16 [768], P('fsdp'), may hold values from -1.75 to 1.75
- out_weight: bfloat16 [768, 768], P('fsdp'), may hold values from -1.75 to 1.75
- out_bias: bfloat16 [768], P('fsdp'), may hold values from -1.75 to 1.75
- second_gain: bfloat16 [768], P('fsdp'), may hold values from 0.099609375 to 1.8984375
- second_bias: bfloat16 [768], P('fsdp'), may hold values from -1.75 to 1.75
- up_weight: bfloat16 [768, 3072], P('fsdp'), may hold values from -0.21875 to 0.21875
- up_bias: bfloat16 [3072], P('fsdp'), may hold values from -1.75 to 1.75
- down_weight: bfloat16 [3072, 768], P('fsdp'), may hold values from -0.21875 to 0.21875
- down_bias: bfloat16 [768], P('fsdp'), may hold values from -1.75 to 1.75
- cotangent: bfloat16 [2, 16, 1024, 768], P(None, ('rep', 'fsdp'), 'seq'), may hold values from -6 to 6
Outputs:
- layer_output: bfloat16 [2, 16, 1024, 768], P(None, ('rep', 'fsdp'), 'seq')
- input_grad: bfloat16 [2, 16, 1024, 768], P(None, ('rep', 'fsdp'), 'seq')
- first_gain_grad: float32 [768], P('fsdp')
- first_bias_grad: float32 [768], P('fsdp')
- query_weight_grad: float32 [768, 768], P('fsdp')
- query_bias_grad: float32 [768], P('fsdp')
- key_weight_grad: float32 [768, 768], P('fsdp')
- value_weight_grad: float32 [768, 768], P('fsdp')
- value_bias_grad: float32 [768], P('fsdp')
- out_weight_grad: float32 [768, 768], P('fsdp')
- out_bias_grad: float32 [768], P('fsdp')
- second_gain_grad: float32 [768], P('fsdp')
- second_bias_grad: float32 [768], P('fsdp')
- up_weight_grad: float32 [768, 3072], P('fsdp')
- up_bias_grad: float32 [3072], P('fsdp')
- down_weight_grad: float32 [3072, 768], P('fsdp')
- down_bias_grad: float32 [768], P('fsdp')
Inputs may be any that keep to these rules, and one draw needn't show every extreme that they name: segment numbers of a sequence never fall; each document is one run of tokens.
All inputs are finite; a program needn't handle non-finite values.
Results may differ from a plain program's by a relative error of at most 0.02.
Values may be sent and summed in bfloat16 or wider, within the bound.
A program may use at most 192 MiB of HBM per device.

v0:
```python
import functools
import jax
import jax.numpy as jnp
from jax import lax
from jax.experimental import pallas as pl
from jax.experimental.pallas import tpu as pltpu
from jax.sharding import PartitionSpec as P

norm_eps = 1e-05

HEADS = 12
HDIM = 64
BLOCK = 64
TQ = 256
TK = 256
NEG = -1e30


def nt(a, b):
    return lax.dot_general(a, b, (((1,), (1,)), ((), ())), preferred_element_type=jnp.float32)


def tn(a, b):
    return lax.dot_general(a, b, (((0,), (0,)), ((), ())), preferred_element_type=jnp.float32)


def nn(a, b):
    return jnp.dot(a, b, preferred_element_type=jnp.float32)


def head_lanes(head):
    lane = lax.broadcasted_iota(jnp.int32, (1, 128), 1)
    return (lane < HDIM) if head == 0 else (lane >= HDIM)


def bias_rows(block_ref, doc_ref, head):
    rows = [
        jnp.broadcast_to(block_ref[0, 0, head, pl.ds(b, 1), :], (BLOCK, 128)) for b in range(TQ // BLOCK)
    ]
    return (jnp.concatenate(rows, axis=0) + doc_ref[0]).astype(jnp.bfloat16)


def unite(whole, own_ref, other_ref, side):
    half = own_ref.shape[1]
    whole[pl.ds(pl.multiple_of(side * half, TK), half), :] = own_ref[0]
    whole[pl.ds(pl.multiple_of((1 - side) * half, TK), half), :] = other_ref[0]


def forward_body(
    span_ref, q_ref, ko_ref, vo_ref, kx_ref, vx_ref, aug_ref, block_ref, doc_ref,
    out_ref, lse_ref, acc_ref, qa_ref, k_all, v_all,
):
    micro, tile = pl.program_id(0), pl.program_id(1)

    @pl.when(tile == 0)
    def _():
        unite(k_all, ko_ref, kx_ref, span_ref[micro, tile, 2])
        unite(v_all, vo_ref, vx_ref, span_ref[micro, tile, 2])

    group = q_ref.shape[2] // HDIM
    for head in range(group):
        cols = pl.ds(head // 2 * 128, 128)
        q_rows = q_ref[0, :, cols].astype(jnp.float32) * 0.125
        masked = jnp.where(head_lanes(head % 2), q_rows, 0.0).astype(jnp.bfloat16)
        qa_ref[head, :, 0:128] = masked
        qa_ref[head, :, 128:256] = bias_rows(block_ref, doc_ref, head)
    acc_ref[...] = jnp.zeros_like(acc_ref)

    def step(j, carry):
        at = pl.ds(pl.multiple_of(j * TK, TK), TK)
        aug = aug_ref[0, at, :]
        scores = []
        for head in range(group):
            cols = pl.ds(head // 2 * 128, 128)
            scores.append(nt(jnp.concatenate([k_all[at, cols], aug], axis=1), qa_ref[head]))
        fresh = []
        probs = []
        for head in range(group):
            top_new = jnp.maximum(carry[head], jnp.max(scores[head], axis=0, keepdims=True))
            probs.append(jnp.exp(scores[head] - top_new).astype(jnp.bfloat16))
            fresh.append(top_new)
        for head in range(group):
            cols = pl.ds(head // 2 * 128, 128)
            v_rows = jnp.where(head_lanes(head % 2), v_all[at, cols], jnp.bfloat16(1.0))
            part = tn(v_rows, probs[head])
            acc_ref[head] = acc_ref[head] * jnp.exp(carry[head] - fresh[head]) + part
        return tuple(fresh)

    state = tuple(jnp.full((1, TQ), -3e38, jnp.float32) for _ in range(group))
    state = lax.fori_loop(span_ref[micro, tile, 0], span_ref[micro, tile, 1], step, state)
    for pair in range(group // 2):
        done = []
        for head in range(2):
            at = pair * 2 + head
            mass = acc_ref[at, pl.ds((1 - head) * HDIM, 1), :]
            done.append(acc_ref[at, pl.ds(head * HDIM, HDIM), :] / mass)
            lse_ref[0, pair, pl.ds(head, 1), :] = state[at] + jnp.log(mass)
        out_ref[0, :, pl.ds(pair * 128, 128)] = jnp.concatenate(done, axis=0).T.astype(out_ref.dtype)


def backward_body(
    micro, carried,
    span_ref, q_ref, ko_ref, vo_ref, kx_ref, vx_ref, aug_ref, block_ref, doc_ref,
    mixed_ref, grad_ref, lse_ref, *rest,
):
    dq_ref, dko_ref, dvo_ref, dkx_ref, dvx_ref = rest[carried:carried + 5]
    dqt_ref, qa_ref, gm_ref, k_acc, v_acc, k_all, v_all = rest[carried + 5:]
    tile = pl.program_id(0)
    side = span_ref[micro, tile, 2]

    @pl.when(tile == 0)
    def _():
        unite(k_all, ko_ref, kx_ref, side)
        unite(v_all, vo_ref, vx_ref, side)
        k_acc[...] = jnp.zeros_like(k_acc)
        v_acc[...] = jnp.zeros_like(v_acc)

    group = q_ref.shape[2] // HDIM
    inner = []
    for pair in range(group // 2):
        cols = pl.ds(pair * 128, 128)
        q_rows = q_ref[0, :, cols].astype(jnp.float32) * 0.125
        grad_rows = grad_ref[0, :, cols].astype(jnp.float32)
        both = (mixed_ref[0, :, cols].astype(jnp.float32) * grad_rows).T
        for half in range(2):
            head = pair * 2 + half
            qa_ref[head, :, 0:128] = jnp.where(head_lanes(half), q_rows, 0.0).astype(jnp.bfloat16)
            qa_ref[head, :, 128:256] = bias_rows(block_ref, doc_ref, head)
            gm_ref[head] = jnp.where(head_lanes(half), grad_rows, 0.0).astype(jnp.bfloat16)
            inner.append(jnp.sum(both[half * HDIM:(half + 1) * HDIM, :], axis=0, keepdims=True))
    dqt_ref[...] = jnp.zeros_like(dqt_ref)

    def step(j, carry):
        at = pl.ds(pl.multiple_of(j * TK, TK), TK)
        aug = aug_ref[0, at, :]
        for chunk in range(0, group, CHUNK):
            heads = range(chunk, min(chunk + CHUNK, group))
            scores, grads, probs, souls = {}, {}, {}, {}
            for head in heads:
                cols = pl.ds(head // 2 * 128, 128)
                scores[head] = nt(jnp.concatenate([k_all[at, cols], aug], axis=1), qa_ref[head])
                grads[head] = nt(v_all[at, cols], gm_ref[head])
            for head in heads:
                weight = jnp.exp(scores[head] - lse_ref[0, head // 2, pl.ds(head % 2, 1), :])
                souls[head] = (weight * (grads[head] - carry[head])).astype(jnp.bfloat16)
                probs[head] = weight.astype(jnp.bfloat16)
            for head in heads:
                cols = pl.ds(head // 2 * 128, 128)
                dv = nn(probs[head], gm_ref[head])
                dk = nn(souls[head], qa_ref[head, :, 0:128])
                dqt = tn(k_all[at, cols], souls[head])
                lanes = pl.ds(head * HDIM, HDIM)
                half = head % 2
                dqt_ref[lanes, :] += dqt[half * HDIM:(half + 1) * HDIM, :]
                if half == 0:
                    dv_low, dk_low = dv, dk
                else:
                    k_acc[at, cols] += dk + dk_low
                    v_acc[at, cols] += dv + dv_low
        return carry

    lax.fori_loop(span_ref[micro, tile, 0], span_ref[micro, tile, 1], step, tuple(inner))
    for pair in range(group // 2):
        cols = pl.ds(pair * 128, 128)
        dq_ref[0, :, cols] = (dqt_ref[cols, :] * 0.125).T.astype(dq_ref.dtype)

    @pl.when(tile == pl.num_programs(0) - 1)
    def _():
        size = dko_ref.shape[1]
        mine = pl.ds(pl.multiple_of(side * size, TK), size)
        theirs = pl.ds(pl.multiple_of((1 - side) * size, TK), size)
        dko_ref[0] = k_acc[mine, :].astype(dko_ref.dtype)
        dvo_ref[0] = v_acc[mine, :].astype(dvo_ref.dtype)
        dkx_ref[0] = k_acc[theirs, :].astype(dkx_ref.dtype)
        dvx_ref[0] = v_acc[theirs, :].astype(dvx_ref.dtype)


CHUNK = 4


def specs(half, length, width, at):
    rows = pl.BlockSpec((1, TQ, width), lambda *i: at(*i) + (0,))
    side = pl.BlockSpec((1, half, width), lambda *i: (at(*i)[0], 0, 0))
    aug = pl.BlockSpec((1, length, 128), lambda *i: (at(*i)[0], 0, 0))
    block = pl.BlockSpec((1, 1, HEADS, TQ // BLOCK, 128), lambda *i: at(*i) + (0, 0, 0))
    doc = pl.BlockSpec((1, TQ, 128), lambda *i: at(*i) + (0,))
    lse = pl.BlockSpec((1, HEADS // 2, 2, TQ), lambda *i: (at(*i)[0], 0, 0, at(*i)[1]))
    return rows, side, aug, block, doc, lse


def attend_forward(span, q, ko, vo, kx, vx, aug, block, doc):
    micro, half, width = q.shape
    length = aug.shape[1]
    rows, side, aug_spec, blk, doc_spec, lse = specs(half, length, width, lambda m, t, s: (m, t))
    return pl.pallas_call(
        forward_body,
        name="attend_forward",
        out_shape=(
            jax.ShapeDtypeStruct((micro, half, width), jnp.bfloat16),
            jax.ShapeDtypeStruct((micro, HEADS // 2, 2, half), jnp.float32),
        ),
        grid_spec=pltpu.PrefetchScalarGridSpec(
            num_scalar_prefetch=1,
            grid=(micro, half // TQ),
            in_specs=[rows] + [side] * 4 + [aug_spec, blk, doc_spec],
            out_specs=(rows, lse),
            scratch_shapes=[
                pltpu.VMEM((HEADS, 128, TQ), jnp.float32),
                pltpu.VMEM((HEADS, TQ, 256), jnp.bfloat16),
                pltpu.VMEM((length, width), jnp.bfloat16),
                pltpu.VMEM((length, width), jnp.bfloat16),
            ],
        ),
        cost_estimate=pl.CostEstimate(flops=20_000_000_000, bytes_accessed=20_000_000, transcendentals=0),
    )(span, q, ko, vo, kx, vx, aug, block, doc)


def attend_backward(step, carried, span, q, ko, vo, kx, vx, aug, block, doc, mixed, grad, lse):
    micro, half, width = q.shape
    length = aug.shape[1]
    rows, side, aug_spec, blk, doc_spec, lse_spec = specs(half, length, width, lambda t, s: (step, t))
    shape = jax.ShapeDtypeStruct((micro, half, width), jnp.bfloat16)
    return pl.pallas_call(
        functools.partial(backward_body, step, len(carried)),
        name="attend_backward",
        out_shape=(shape,) * 5,
        grid_spec=pltpu.PrefetchScalarGridSpec(
            num_scalar_prefetch=1,
            grid=(half // TQ,),
            in_specs=[rows] + [side] * 4 + [aug_spec, blk, doc_spec, rows, rows, lse_spec]
            + [pl.BlockSpec(memory_space=pl.ANY)] * len(carried),
            out_specs=(rows,) + (side,) * 4,
            scratch_shapes=[
                pltpu.VMEM((width, TQ), jnp.float32),
                pltpu.VMEM((HEADS, TQ, 256), jnp.bfloat16),
                pltpu.VMEM((HEADS, TQ, 128), jnp.bfloat16),
                pltpu.VMEM((length, width), jnp.float32),
                pltpu.VMEM((length, width), jnp.float32),
                pltpu.VMEM((length, width), jnp.bfloat16),
                pltpu.VMEM((length, width), jnp.bfloat16),
            ],
        ),
        input_output_aliases={12 + i: i for i in range(len(carried))},
        cost_estimate=pl.CostEstimate(flops=20_000_000_000, bytes_accessed=20_000_000, transcendentals=0),
    )(span, q, ko, vo, kx, vx, aug, block, doc, mixed, grad, lse, *carried)


def tables(segment, rand_blocks, side, half):
    micro, length = segment.shape
    blocks = length // BLOCK
    mine = half // BLOCK
    tiles = half // TQ
    lane = lax.broadcasted_iota(jnp.int32, (1, 1, 128), 2)
    own = lax.dynamic_slice_in_dim(segment, side * half, half, axis=1)
    place = lax.broadcasted_iota(jnp.int32, (1, length, 1), 1) // BLOCK
    aug = ((lane == place) | (lane == segment[:, :, None] + blocks)).astype(jnp.bfloat16)
    doc = jnp.where((lane >= blocks) & (lane < blocks + 4) & (lane != own[:, :, None] + blocks), NEG, 0.0)
    q_block = side * mine + lax.broadcasted_iota(jnp.int32, (1, 1, mine, 1), 2)
    k_block = lax.broadcasted_iota(jnp.int32, (1, 1, 1, 128), 3)
    chosen = lax.dynamic_slice_in_dim(rand_blocks, side * mine, mine, axis=2)
    allowed = (jnp.abs(q_block - k_block) <= 1) | (k_block == 0) | (k_block == blocks - 1)
    allowed = allowed | (q_block == 0) | (q_block == blocks - 1) | (k_block >= blocks)
    for pick in range(rand_blocks.shape[3]):
        allowed = allowed | (chosen[:, :, :, pick:pick + 1] == k_block)
    block = jnp.where(allowed, 0.0, NEG).astype(jnp.float32)
    block = jnp.moveaxis(block.reshape(micro, HEADS, tiles, mine // tiles, 128), 2, 1)
    edges = own.reshape(micro, tiles, TQ)
    first, last = edges[:, :, :1], edges[:, :, TQ - 1:]
    begin = jnp.sum((segment[:, None, :] < first).astype(jnp.int32), axis=-1)
    end = jnp.sum((segment[:, None, :] <= last).astype(jnp.int32), axis=-1)
    span = jnp.stack([begin // TK, (end + TK - 1) // TK, jnp.full_like(begin, side)], axis=-1)
    return span, aug, block, doc.astype(jnp.float32)


MESH = pl.DeviceIdType.MESH
GROUPS = 3


def place():
    rep, shard, side = lax.axis_index("rep"), lax.axis_index("fsdp"), lax.axis_index("seq")
    quad = lax.rem(rep, 4)
    across, along = lax.rem(quad, 2), quad // 2
    near = (1 - 2 * across, 2 - 4 * along)
    return rep, shard, side, quad, near


def chunk(refs, group, shard, quad, side, rows, half=None):
    width = 768 if half is None else 384
    offset = 0 if half is None else half * 384
    low = side * rows
    if group == 0:
        return refs[0].at[quad, pl.ds(pl.multiple_of(shard * (2 * rows) + low, 16), rows), pl.ds(offset, width)]
    if group == 1:
        at = pl.multiple_of(shard * (2 * rows) + low, 16)
        return refs[1].at[pl.ds(at, rows), pl.ds(pl.multiple_of(quad * 768 + offset, 128), width)]
    at = pl.multiple_of(shard * (8 * rows) + quad * (2 * rows) + low, 16)
    return refs[2].at[pl.ds(at, rows), pl.ds(offset, width)]


def greet(peers):
    barrier = pltpu.get_barrier_semaphore()
    for peer in peers:
        pl.semaphore_signal(barrier, inc=1, device_id=peer, device_id_type=MESH)
    pl.semaphore_wait(barrier, len(peers))


def remote(src, dst, send, recv, peer):
    return pltpu.make_async_remote_copy(
        src_ref=src, dst_ref=dst, send_sem=send, recv_sem=recv, device_id=peer, device_id_type=MESH
    )


def gather_body(
    shards, rows, qkvo_in, up_in, down_in, vec_in, x_in,
    qkvo_out, up_out, down_out, vec_out, normed_out, q_out, k_out, v_out, kx_out, vx_out,
    qkvo_stage, up_stage, down_stage, vec_all, weights, normed, results,
    in_sem, out_sem, z_send, z_recv, x_send, x_recv, y_send, y_recv, d_send, d_recv, c_send, c_recv,
    load_sem, save_sem, swap_send, swap_recv,
):
    rep, shard, side, quad, (dx, dy) = place()
    ins, outs = (qkvo_in, up_in, down_in), (qkvo_out, up_out, down_out)
    stages = (qkvo_stage, up_stage, down_stage)
    x_peer, y_peer, partner = (rep + dx, shard, side), (rep + dy, shard, side), (rep, shard, 1 - side)
    z_peers = [(rep, lax.rem(shard + k, shards), side) for k in range(1, shards)]
    for i, src in enumerate(ins):
        pltpu.make_async_copy(src, stages[i], in_sem.at[i]).start()
    greet(z_peers + [x_peer, y_peer, partner])
    sent = []

    def go(copy):
        copy.start()
        sent.append(copy)

    for g in range(GROUPS):
        for k in range(1, shards):
            go(remote(
                chunk(ins, g, 0, quad, side, rows), chunk(outs, g, shard, quad, side, rows),
                z_send.at[g, k - 1], z_recv.at[g, shards - k - 1], z_peers[k - 1],
            ))
        if g == 0:
            for k in range(1, shards):
                go(remote(
                    vec_in, vec_all.at[k - 1],
                    z_send.at[GROUPS, k - 1], z_recv.at[GROUPS, k - 1], z_peers[k - 1],
                ))
    owned = (
        qkvo_out.at[:, pl.ds(pl.multiple_of(shard * 2 * rows, 16), 2 * rows), :],
        up_out.at[pl.ds(pl.multiple_of(shard * 2 * rows, 16), 2 * rows), :],
        down_out.at[pl.ds(pl.multiple_of(shard * 8 * rows, 16), 8 * rows), :],
    )
    local = []
    for i, src in enumerate(ins):
        pltpu.make_async_copy(src, stages[i], in_sem.at[i]).wait()
        copy = pltpu.make_async_copy(stages[i], owned[i], out_sem.at[i])
        copy.start()
        local.append(copy)

    def piece(g, k, member, core, half=None):
        return chunk(outs, g, lax.rem(shard + k, shards), member, core, rows, half)

    def hop(g, k, member, core, send, recv, peer, half=None):
        ref = piece(g, k, member, core, half)
        return remote(ref, ref, send, recv, peer)

    x_quad, y_quad, d_quad = quad + dx, quad + dy, quad + dx + dy

    def straight(g):
        for k in range(1, shards):
            hop(g, k, quad, side, z_send.at[g, k - 1], z_recv.at[g, k - 1], z_peers[k - 1]).wait_recv()
            go(hop(g, k, quad, side, x_send.at[g, k - 1], x_recv.at[g, k - 1], x_peer))
            go(hop(g, k, quad, side, y_send.at[g, k - 1], y_recv.at[g, k - 1], y_peer))
            go(hop(g, k, quad, side, c_send.at[g, k - 1, 0], c_recv.at[g, k - 1, 0], partner))

    def turn(g):
        for k in range(1, shards):
            hop(g, k, x_quad, side, x_send.at[g, k - 1], x_recv.at[g, k - 1], x_peer).wait_recv()
            go(hop(g, k, x_quad, side, d_send.at[g, k - 1, 1], d_recv.at[g, k - 1, 1], y_peer, 1))
            go(hop(g, k, x_quad, side, c_send.at[g, k - 1, 1], c_recv.at[g, k - 1, 1], partner))
            hop(g, k, y_quad, side, y_send.at[g, k - 1], y_recv.at[g, k - 1], y_peer).wait_recv()
            go(hop(g, k, y_quad, side, d_send.at[g, k - 1, 0], d_recv.at[g, k - 1, 0], x_peer, 0))
            go(hop(g, k, y_quad, side, c_send.at[g, k - 1, 2], c_recv.at[g, k - 1, 2], partner))

    def corner(g):
        for k in range(1, shards):
            hop(g, k, d_quad, side, d_send.at[g, k - 1, 0], d_recv.at[g, k - 1, 0], x_peer, 0).wait_recv()
            hop(g, k, d_quad, side, d_send.at[g, k - 1, 1], d_recv.at[g, k - 1, 1], y_peer, 1).wait_recv()
            go(hop(g, k, d_quad, side, c_send.at[g, k - 1, 3], c_recv.at[g, k - 1, 3], partner))

    def gathered(g):
        for k in range(1, shards):
            for i, member in enumerate((quad, x_quad, y_quad, d_quad)):
                hop(g, k, member, 1 - side, c_send.at[g, k - 1, i], c_recv.at[g, k - 1, i], partner).wait_recv()

    def save(i, target):
        copy = pltpu.make_async_copy(normed if i == 3 else results.at[i], target, save_sem.at[i])
        copy.start()
        local.append(copy)

    def norm(step, carry):
        at = pl.ds(pl.multiple_of(step * STEP, STEP), STEP)
        values = x_in[at, :].astype(jnp.float32)
        centre = values - jnp.mean(values, axis=-1, keepdims=True)
        scale = lax.rsqrt(jnp.mean(centre * centre, axis=-1, keepdims=True) + norm_eps)
        normed[at, :] = (centre * scale * vec_out[0:1, :] + vec_out[1:2, :]).astype(normed.dtype)
        return carry

    def project(i, row):
        pltpu.make_async_copy(qkvo_out.at[i], weights.at[i], load_sem.at[i]).wait()

        def step(j, carry):
            at = pl.ds(pl.multiple_of(j * STEP, STEP), STEP)
            product = nn(normed[at, :], weights[i])
            if row is not None:
                product = product + vec_out[row:row + 1, :]
            results[i, at, :] = product.astype(results.dtype)
            return carry
        lax.fori_loop(0, normed.shape[0] // STEP, step, 0)

    def exchange(i, target):
        copy = remote(results.at[i], target, swap_send.at[i - 1], swap_recv.at[i - 1], partner)
        copy.start()
        return copy

    straight(0)
    for k in range(1, shards):
        remote(
            vec_in, vec_all.at[k - 1], z_send.at[GROUPS, k - 1], z_recv.at[GROUPS, k - 1], z_peers[k - 1]
        ).wait_recv()
    total = vec_in[...].astype(jnp.float32)
    for k in range(1, shards):
        total = total + vec_all[k - 1].astype(jnp.float32)
    vec_out[...] = total
    lax.fori_loop(0, normed.shape[0] // STEP // 2, norm, 0)
    turn(0)
    lax.fori_loop(normed.shape[0] // STEP // 2, normed.shape[0] // STEP, norm, 0)
    save(3, normed_out)
    straight(1)
    corner(0)
    turn(1)
    local[0].wait()
    gathered(0)
    for i in (1, 2, 0):
        pltpu.make_async_copy(qkvo_out.at[i], weights.at[i], load_sem.at[i]).start()
    straight(2)
    project(1, None)
    keys = exchange(1, kx_out)
    save(1, k_out)
    corner(1)
    project(2, 3)
    values = exchange(2, vx_out)
    save(2, v_out)
    turn(2)
    project(0, 2)
    save(0, q_out)
    corner(2)
    gathered(1)
    gathered(2)
    keys.wait()
    values.wait()
    for copy in sent:
        copy.wait_send()
    for copy in local[1:]:
        copy.wait()


STEP = 256


def gather_weights(shards, qkvo, up, down, vec, x):
    rows = qkvo.shape[1] // 2
    model = qkvo.shape[2]
    hidden = up.shape[1]
    any_space = pl.BlockSpec(memory_space=pl.ANY)
    vmem_space = pl.BlockSpec(memory_space=pltpu.VMEM)
    dma = pltpu.SemaphoreType.DMA
    low = jnp.bfloat16
    token = jax.ShapeDtypeStruct(x.shape, low)
    return pl.pallas_call(
        functools.partial(gather_body, shards, rows),
        name="gather_weights",
        out_shape=(
            jax.ShapeDtypeStruct((4, model, model), low),
            jax.ShapeDtypeStruct((model, hidden), low),
            jax.ShapeDtypeStruct((hidden, model), low),
            jax.ShapeDtypeStruct(vec.shape, jnp.float32),
        )
        + (token,) * 6,
        in_specs=[any_space] * 3 + [vmem_space] * 2,
        out_specs=(any_space,) * 3 + (vmem_space,) + (any_space,) * 6,
        scratch_shapes=[
            pltpu.VMEM(qkvo.shape, low), pltpu.VMEM(up.shape, low), pltpu.VMEM(down.shape, low),
            pltpu.VMEM((shards - 1,) + vec.shape, low),
            pltpu.VMEM((3, model, model), low),
            pltpu.VMEM(x.shape, low),
            pltpu.VMEM((3,) + x.shape, low),
            dma((3,)), dma((3,)),
            dma((GROUPS + 1, shards - 1)), dma((GROUPS + 1, shards - 1)),
        ]
        + [dma((GROUPS, shards - 1))] * 4
        + [dma((GROUPS, shards - 1, 2))] * 2
        + [dma((GROUPS, shards - 1, 4))] * 2
        + [dma((3,)), dma((4,)), dma((2,)), dma((2,))],
        compiler_params=pltpu.CompilerParams(
            collective_id=0, has_side_effects=True, vmem_limit_bytes=50_000_000
        ),
    )(qkvo, up, down, vec, x)


def add_into(out_ref, refs):
    total = refs[0][...].astype(jnp.float32)
    for ref in refs[1:]:
        total = total + ref[...].astype(jnp.float32)
    out_ref[...] = total.astype(out_ref.dtype)


def normal_parts(values):
    phi = 0.5 + 0.5 * lax.erf(values * 0.7071067811865476)
    return phi, values * (jnp.exp(-0.5 * values * values) * 0.3989422804014327)


def middle_body(
    shards, rows,
    mixed_in, x_in, grad_in, qkvo_in, up_w_in, down_w_in, vec_in,
    result_out, attn_out, mixed_out, d_out_out, up_out, down_out, sums_out,
    mixed, x, grad, out_w, up_w, down_w, middle, normed, turned, hidden, slope,
    up_grad, down_grad, up_mate, down_mate, up_first, down_first, up_second, down_second,
    load_sem, save_sem, uc_send, uc_recv, dc_send, dc_recv, f_send, f_recv, s_send, s_recv,
):
    rep, shard, side, quad, (dx, dy) = place()
    partner = (rep, shard, 1 - side)
    low, wide = jnp.bfloat16, jnp.float32
    steps = x.shape[0] // STEP
    model = x.shape[1]
    width = 8 * rows
    loads = [
        pltpu.make_async_copy(src, dst, load_sem.at[i])
        for i, (src, dst) in enumerate(((mixed_in, mixed), (x_in, x), (qkvo_in.at[3], out_w), (grad_in, grad)))
    ]
    for f in range(shards):
        at = pl.ds(f * width, width)
        loads.append(pltpu.make_async_copy(up_w_in.at[:, at], up_w.at[f], load_sem.at[4 + f]))
        loads.append(pltpu.make_async_copy(down_w_in.at[at, :], down_w.at[f], load_sem.at[4 + shards + f]))
    for load in loads:
        load.start()
    greet([(rep + dx, shard, side), (rep + dy, shard, side), partner])
    firsts, seconds = (up_first, down_first), (up_second, down_second)

    def row(i):
        return vec_in[i:i + 1, :]

    def block(j):
        return pl.ds(pl.multiple_of(j * STEP, STEP), STEP)

    def part(g, f, m):
        return up_grad.at[m, f, side] if g == 0 else down_grad.at[f, side, m]

    def mate(g, f, m):
        return up_mate.at[m, f] if g == 0 else down_mate.at[f, m]

    def flip_way(f, second):
        odd = lax.rem(f + second, 2)
        return dx + odd * (dy - dx)

    def up_cross(m):
        return remote(up_grad.at[m, :, 1 - side], up_mate.at[m], uc_send.at[m], uc_recv.at[m], partner)

    def down_cross(f):
        return remote(down_grad.at[f, 1 - side], down_mate.at[f], dc_send.at[f], dc_recv.at[f], partner)

    def f_copy(g, f, slot):
        way = flip_way(f, 0)
        member = quad + way if slot == 0 else quad + dx + dy
        return remote(part(g, f, member), firsts[g].at[f, slot], f_send.at[g, f, slot], f_recv.at[g, f, slot], (rep + way, shard, side))

    def s_copy(g, f):
        way = flip_way(f, 1)
        return remote(part(g, f, quad + way), seconds[g].at[f], s_send.at[g, f], s_recv.at[g, f], (rep + way, shard, side))

    def first_go(g, f):
        for slot in range(2):
            f_copy(g, f, slot).start()

    def down_merge(f):
        down_cross(f).wait_recv()
        for m in range(4):
            add_into(part(1, f, m), (part(1, f, m), mate(1, f, m)))
        first_go(1, f)

    def up_merge(m):
        up_cross(m).wait_recv()

        def step(f, carry):
            add_into(part(0, f, m), (part(0, f, m), mate(0, f, m)))
            return carry
        lax.fori_loop(0, shards, step, 0)

    def each(body):
        def step(f, carry):
            body(f)
            return carry
        lax.fori_loop(0, shards, step, 0)

    def fold(g):
        def body(f):
            for slot in range(2):
                f_copy(g, f, slot).wait()
                member = quad if slot == 0 else quad + flip_way(f, 1)
                add_into(part(g, f, member), (part(g, f, member), firsts[g].at[f, slot]))
            s_copy(g, f).start()
        each(body)

    def settle(g, target):
        def body(f):
            s_copy(g, f).wait()
            add_into(target.at[f], (part(g, f, quad), seconds[g].at[f]))
        each(body)

    saves = []

    def save(src, dst):
        copy = pltpu.make_async_copy(src, dst, save_sem.at[len(saves)])
        copy.start()
        saves.append(copy)

    for load in loads[:3]:
        load.wait()

    def attend_out(j, carry):
        at = block(j)
        values = x[at, :].astype(wide) + nn(mixed[at, :], out_w[...]) + row(4)
        middle[at, :] = values
        centre = values - jnp.mean(values, axis=-1, keepdims=True)
        scale = lax.rsqrt(jnp.mean(centre * centre, axis=-1, keepdims=True) + norm_eps)
        out = centre * scale * row(5) + row(6)
        normed[at, :] = out.astype(low)
        turned[:, at] = out.T.astype(low)
        return carry
    lax.fori_loop(0, steps, attend_out, 0)
    for load in loads[3:]:
        load.wait()

    def bias_at(f):
        first = f * width
        return pl.ds(8 + first // model, 1), pl.ds(pl.multiple_of(lax.rem(first, model), 128), width)

    def expand(f):
        bias = vec_in[bias_at(f)]

        def step(j, carry):
            at = block(j)
            inner = nn(normed[at, :], up_w[f]) + bias
            phi, bump = normal_parts(inner)
            hidden[f, at, :] = (inner * phi).astype(low)
            slope[f, at, :] = (phi + bump).astype(low)
            return carry
        lax.fori_loop(0, steps, step, 0)
        down_grad[f] = tn(hidden[f], grad[...]).astype(low).reshape(2, 4, rows, model)
        down_cross(f).start()

        @pl.when(f > 0)
        def _():
            down_merge(f - 1)
    each(expand)

    def contract(m):
        for h in range(model // width):
            f = m * (model // width) + h

            def step(j, total, f=f):
                at = block(j)
                value = (nt(grad[at, :], down_w[f]) * slope[f, at, :].astype(wide)).astype(low)
                slope[f, at, :] = value
                return total + jnp.sum(value.astype(wide), axis=0, keepdims=True)
            sums_out[bias_at(f)] = lax.fori_loop(0, steps, step, jnp.zeros((1, width), wide))
            product = nn(turned[...], slope[f]).astype(low)
            up_grad[m, :, :, :, pl.ds(h * width, width)] = product.reshape(shards, 2, rows, width)
        up_cross(m).start()

        @pl.when(m == 0)
        def _():
            down_merge(shards - 1)

        @pl.when(m > 0)
        def _():
            up_merge(m - 1)

    def contract_step(m, carry):
        contract(m)
        return carry
    lax.fori_loop(0, 4, contract_step, 0)
    fold(1)
    up_merge(3)
    each(lambda f: first_go(0, f))

    def finish(j, carry):
        at = block(j)
        total = middle[at, :] + row(7)
        for f in range(shards):
            total = total + nn(hidden[f, at, :], down_w[f])
        x[at, :] = total.astype(low)
        return carry
    lax.fori_loop(0, steps, finish, 0)
    save(x, result_out)

    def back(j, carry):
        gain_sum, bias_sum, attn_sum, grad_sum = carry
        at = block(j)
        error = nt(slope[0, at, :], up_w[0])
        for f in range(1, shards):
            error = error + nt(slope[f, at, :], up_w[f])
        values = middle[at, :]
        centre = values - jnp.mean(values, axis=-1, keepdims=True)
        scale = lax.rsqrt(jnp.mean(centre * centre, axis=-1, keepdims=True) + norm_eps)
        unit = centre * scale
        scaled = error * row(5)
        mean_one = jnp.mean(scaled, axis=-1, keepdims=True)
        mean_two = jnp.mean(scaled * unit, axis=-1, keepdims=True)
        upstream = grad[at, :].astype(wide)
        attn = (upstream + scale * (scaled - mean_one - unit * mean_two)).astype(low)
        grad[at, :] = attn
        normed[at, :] = nt(attn, out_w[...]).astype(low)
        column = lambda array: jnp.sum(array, axis=0, keepdims=True)
        return (
            gain_sum + column(error * unit), bias_sum + column(error),
            attn_sum + column(attn.astype(wide)), grad_sum + column(upstream),
        )
    zero = jnp.zeros((1, model), wide)
    sums = lax.fori_loop(0, steps // 2, back, (zero,) * 4)
    fold(0)
    sums = lax.fori_loop(steps // 2, steps, back, sums)
    save(normed, mixed_out)
    save(grad, attn_out)
    for i, value in enumerate(sums):
        sums_out[i:i + 1, :] = value
    sums_out[4:8, :] = jnp.zeros((4, model), wide)
    sums_out[12:16, :] = jnp.zeros((4, model), wide)
    settle(1, down_out)
    out_w[...] = tn(mixed[...], grad[...]).astype(low)
    save(out_w, d_out_out)
    settle(0, up_out)
    for m in range(4):
        up_cross(m).wait_send()
    each(lambda f: down_cross(f).wait_send())
    for copy in saves:
        copy.wait()


def middle_layer(shards, mixed, x, grad, qkvo, up_w, down_w, vec):
    tokens, model = x.shape
    hidden = up_w.shape[1]
    rows = model // shards // 2
    width = 8 * rows
    any_space = pl.BlockSpec(memory_space=pl.ANY)
    vmem_space = pl.BlockSpec(memory_space=pltpu.VMEM)
    dma = pltpu.SemaphoreType.DMA
    low, wide = jnp.bfloat16, jnp.float32
    token = jax.ShapeDtypeStruct((tokens, model), low)
    flat = pltpu.VMEM((tokens, model), low)
    return pl.pallas_call(
        functools.partial(middle_body, shards, rows),
        name="middle_layer",
        out_shape=(
            token, token, token,
            jax.ShapeDtypeStruct((model, model), low),
            jax.ShapeDtypeStruct((shards, rows, model), low),
            jax.ShapeDtypeStruct((shards, rows, model), low),
            jax.ShapeDtypeStruct((16, model), wide),
        ),
        in_specs=[any_space] * 6 + [vmem_space],
        out_specs=(any_space,) * 4 + (vmem_space,) * 3,
        scratch_shapes=[
            flat, flat, flat,
            pltpu.VMEM((model, model), low),
            pltpu.VMEM((shards, model, width), low),
            pltpu.VMEM((shards, width, model), low),
            pltpu.VMEM((tokens, model), wide),
            flat,
            pltpu.VMEM((model, tokens), low),
            pltpu.VMEM((shards, tokens, width), low),
            pltpu.VMEM((shards, tokens, width), low),
            pltpu.VMEM((4, shards, 2, rows, model), low),
            pltpu.VMEM((shards, 2, 4, rows, model), low),
            pltpu.VMEM((4, shards, rows, model), low),
            pltpu.VMEM((shards, 4, rows, model), low),
            pltpu.VMEM((shards, 2, rows, model), low),
            pltpu.VMEM((shards, 2, rows, model), low),
            pltpu.VMEM((shards, rows, model), low),
            pltpu.VMEM((shards, rows, model), low),
            dma((4 + 2 * shards,)), dma((4,)),
            dma((4,)), dma((4,)), dma((shards,)), dma((shards,)),
            dma((2, shards, 2)), dma((2, shards, 2)), dma((2, shards)), dma((2, shards)),
        ],
        compiler_params=pltpu.CompilerParams(
            collective_id=2, has_side_effects=True, vmem_limit_bytes=66_000_000
        ),
    )(mixed, x, grad, qkvo, up_w, down_w, vec)


def final_body(
    shards, quads, rows,
    dq_in, dk_in, dv_in, dkx_in, dvx_in, normed_in, x_in, attn_in, w_in, d_out_in, up_in, down_in, vec_in, small_in,
    qkvo_out, up_out, down_out, vec_out, input_out,
    dq, dk, dv, dkx, dvx, normed, turned, x, attn, weights, grads, mate, first, second,
    last, last_up, last_down, ring, ring_up, ring_down, full, full_up, full_down, vec_sum, vec_mate, vec_ring,
    load_sem, save_sem, w_send, w_recv, c_send, c_recv, f_send, f_recv, s_send, s_recv, z_send, z_recv, q_send, q_recv,
    x_send, x_recv, y_send, y_recv, d_send, d_recv, g_send, g_recv, out_sem, v_send, v_recv,
):
    rep, shard, side, quad, (dx, dy) = place()
    low, wide = jnp.bfloat16, jnp.float32
    steps = x.shape[0] // STEP
    model = x.shape[1]
    x_peer, y_peer, partner = (rep + dx, shard, side), (rep + dy, shard, side), (rep, shard, 1 - side)
    x_quad, y_quad, d_quad = quad + dx, quad + dy, quad + dx + dy
    z_peers = [(rep, lax.rem(shard + k, shards), side) for k in range(1, shards)]
    q_peers = [(lax.rem(rep + 4 * k, 4 * quads), shard, side) for k in range(1, quads)]
    loads = [
        pltpu.make_async_copy(src, dst, load_sem.at[i])
        for i, (src, dst) in enumerate((
            (normed_in, normed), (dq_in, dq), (d_out_in, grads.at[3]), (dk_in, dk), (dv_in, dv),
            (w_in.at[0], weights.at[0]), (w_in.at[1], weights.at[1]), (w_in.at[2], weights.at[2]),
            (x_in, x), (attn_in, attn),
        ))
    ]
    for load in loads:
        load.start()
    greet(z_peers + q_peers + [x_peer, y_peer, partner])
    swaps = [
        remote(src, dst, w_send.at[i], w_recv.at[i], partner)
        for i, (src, dst) in enumerate(((dkx_in, dkx), (dvx_in, dvx)))
    ]
    for swap in swaps:
        swap.start()
    fulls, lasts, rings = (full, full_up, full_down), (last, last_up, last_down), (ring, ring_up, ring_down)

    def block(j):
        return pl.ds(pl.multiple_of(j * STEP, STEP), STEP)

    def part(f, m):
        return grads.at[m, f, side]

    def source(g, f):
        return (part(f, quad), up_in.at[f], down_in.at[f])[g]

    def flip_way(f, after):
        odd = lax.rem(f + after, 2)
        return dx + odd * (dy - dx)

    def cross(m):
        return remote(grads.at[m, :, 1 - side], mate.at[m], c_send.at[m], c_recv.at[m], partner)

    def f_copy(f, slot):
        way = flip_way(f, 0)
        member = quad + way if slot == 0 else d_quad
        return remote(part(f, member), first.at[f, slot], f_send.at[f, slot], f_recv.at[f, slot], (rep + way, shard, side))

    def s_copy(f):
        way = flip_way(f, 1)
        return remote(part(f, quad + way), second.at[f], s_send.at[f], s_recv.at[f], (rep + way, shard, side))

    def z_copy(g, k):
        return remote(
            source(g, lax.rem(shard + k, shards)), lasts[g].at[shards - k - 1],
            z_send.at[g, k - 1], z_recv.at[g, shards - k - 1], z_peers[k - 1],
        )

    def z_wait(g, k):
        remote(source(g, shard), lasts[g].at[k - 1], z_send.at[g, k - 1], z_recv.at[g, k - 1], z_peers[k - 1]).wait_recv()

    def vec_copy(src, i, peer, slot=None):
        return remote(src, vec_mate.at[i if slot is None else slot], v_send.at[i], v_recv.at[i if slot is None else slot], peer)

    def spread(g, member, send, recv, peer, half=None, core=None):
        core = side if core is None else core
        ref = fulls[g].at[core, member]
        if half is not None:
            width = ref.shape[-1] // 2
            ref = fulls[g].at[core, member, :, pl.ds(half * width, width)]
        return remote(ref, ref, send, recv, peer)

    def swirl(g):
        mine = fulls[g].at[side, quad]
        for k in range(1, shards):
            z_wait(g, k)
        add_into(mine, [source(g, shard)] + [lasts[g].at[k] for k in range(shards - 1)])
        for k in range(1, quads):
            remote(mine, rings[g].at[quads - k - 1], q_send.at[g, k - 1], q_recv.at[g, quads - k - 1], q_peers[k - 1]).start()
        for k in range(1, quads):
            remote(mine, rings[g].at[k - 1], q_send.at[g, k - 1], q_recv.at[g, k - 1], q_peers[k - 1]).wait()
        if quads > 1:
            add_into(mine, [mine] + [rings[g].at[k] for k in range(quads - 1)])
        spread(g, quad, x_send.at[g], x_recv.at[g], x_peer).start()
        spread(g, quad, y_send.at[g], y_recv.at[g], y_peer).start()
        spread(g, quad, g_send.at[g, 0], g_recv.at[g, 0], partner).start()

    def turn(g):
        spread(g, x_quad, x_send.at[g], x_recv.at[g], x_peer).wait_recv()
        spread(g, x_quad, d_send.at[g, 1], d_recv.at[g, 1], y_peer, 1).start()
        spread(g, x_quad, g_send.at[g, 1], g_recv.at[g, 1], partner).start()
        spread(g, y_quad, y_send.at[g], y_recv.at[g], y_peer).wait_recv()
        spread(g, y_quad, d_send.at[g, 0], d_recv.at[g, 0], x_peer, 0).start()
        spread(g, y_quad, g_send.at[g, 2], g_recv.at[g, 2], partner).start()

    def corner(g):
        spread(g, d_quad, d_send.at[g, 0], d_recv.at[g, 0], x_peer, 0).wait_recv()
        spread(g, d_quad, d_send.at[g, 1], d_recv.at[g, 1], y_peer, 1).wait_recv()
        spread(g, d_quad, g_send.at[g, 3], g_recv.at[g, 3], partner).start()

    def target(g, m, core):
        if g == 0:
            return qkvo_out.at[m, pl.ds(core * rows, rows), :]
        if g == 1:
            return up_out.at[pl.ds(core * rows, rows), pl.ds(m * model, model)]
        return down_out.at[pl.ds((core * 4 + m) * rows, rows), :]

    def put(g, m, core):
        return pltpu.make_async_copy(fulls[g].at[core, m], target(g, m, core), out_sem.at[g, m, core])

    def finish(g):
        for i, member in enumerate((quad, x_quad, y_quad, d_quad)):
            spread(g, member, g_send.at[g, i], g_recv.at[g, i], partner, core=1 - side).wait_recv()
        for m in range(4):
            for core in range(2):
                put(g, m, core).start()

    def each(body):
        def step(f, carry):
            body(f)
            return carry
        lax.fori_loop(0, shards, step, 0)

    def column(array):
        return jnp.sum(array.astype(wide), axis=0, keepdims=True)

    def weight_grad(m, errors):
        grads[m] = nn(turned[...], errors[...]).astype(low).reshape(shards, 2, rows, model)
        cross(m).start()

    def merge(m):
        cross(m).wait_recv()

        def step(f, carry):
            add_into(part(f, m), (part(f, m), mate.at[m, f]))
            return carry
        lax.fori_loop(0, shards, step, 0)

    for g in (2, 1):
        for k in range(1, shards):
            z_copy(g, k).start()
    loads[2].wait()
    cross(3).start()
    loads[0].wait()

    def flip(j, carry):
        turned[:, block(j)] = normed[block(j), :].astype(wide).T.astype(low)
        return carry
    lax.fori_loop(0, steps, flip, 0)
    loads[1].wait()
    weight_grad(0, dq)
    merge(3)
    for i, (mine, theirs) in enumerate(((dk, dkx), (dv, dvx))):
        loads[3 + i].wait()
        swaps[i].wait_recv()

        def join(j, carry, mine=mine, theirs=theirs):
            mine[block(j), :] = (mine[block(j), :].astype(wide) + theirs[block(j), :].astype(wide)).astype(low)
            return carry
        lax.fori_loop(0, steps, join, 0)
        weight_grad(1 + i, mine)
        merge(i)
    merge(2)

    def begin(f):
        for slot in range(2):
            f_copy(f, slot).start()
    each(begin)
    for load in loads[5:]:
        load.wait()

    def back(j, carry):
        at = block(j)
        error = nt(dq[at, :], weights[0]) + nt(dk[at, :], weights[1]) + nt(dv[at, :], weights[2])
        values = x[at, :].astype(wide)
        centre = values - jnp.mean(values, axis=-1, keepdims=True)
        scale = lax.rsqrt(jnp.mean(centre * centre, axis=-1, keepdims=True) + norm_eps)
        unit = centre * scale
        scaled = error * vec_in[0:1, :]
        mean_one = jnp.mean(scaled, axis=-1, keepdims=True)
        mean_two = jnp.mean(scaled * unit, axis=-1, keepdims=True)
        x[at, :] = (attn[at, :].astype(wide) + scale * (scaled - mean_one - unit * mean_two)).astype(low)
        gain, bias, query, value = carry
        return gain + column(error * unit), bias + column(error), query + column(dq[at, :]), value + column(dv[at, :])
    zero = jnp.zeros((1, model), wide)
    sums = lax.fori_loop(0, steps, back, (zero,) * 4)
    save = pltpu.make_async_copy(x, input_out, save_sem.at[0])
    save.start()
    vec_sum[...] = small_in[...]
    for i, value in enumerate(sums):
        vec_sum[4 + i:5 + i, :] = value
    vec_copy(vec_sum, 0, partner).start()

    def fold(f):
        for slot in range(2):
            f_copy(f, slot).wait()
            member = quad if slot == 0 else quad + flip_way(f, 1)
            add_into(part(f, member), (part(f, member), first.at[f, slot]))
        s_copy(f).start()
    each(fold)
    vec_copy(vec_sum, 0, partner).wait()
    vec_sum[...] = vec_sum[...] + vec_mate[0]
    vec_copy(vec_sum, 1, x_peer).start()
    swirl(2)
    swirl(1)

    def settle(f):
        s_copy(f).wait()
        add_into(part(f, quad), (part(f, quad), second.at[f]))
    each(settle)
    for k in range(1, shards):
        z_copy(0, k).start()
    vec_copy(vec_sum, 1, x_peer).wait()
    vec_sum[...] = vec_sum[...] + vec_mate[1]
    vec_copy(vec_sum, 2, y_peer).start()
    turn(2)
    turn(1)
    vec_copy(vec_sum, 2, y_peer).wait()
    vec_sum[...] = vec_sum[...] + vec_mate[2]
    for k in range(1, shards):
        vec_copy(vec_sum, 2 + k, z_peers[k - 1], 2 + shards - k).start()
    corner(2)
    corner(1)
    swirl(0)
    finish(2)
    finish(1)
    total = vec_sum[...]
    for k in range(1, shards):
        vec_copy(vec_sum, 2 + k, z_peers[k - 1]).wait()
        total = total + vec_mate[2 + k]
    vec_ring[0] = total
    base = 2 + shards
    for k in range(1, quads):
        remote(vec_ring.at[0], vec_ring.at[quads - k], v_send.at[base + k], v_recv.at[base + quads - k], q_peers[k - 1]).start()
    for k in range(1, quads):
        remote(vec_ring.at[0], vec_ring.at[k], v_send.at[base + k], v_recv.at[base + k], q_peers[k - 1]).wait()
        total = total + vec_ring[k]
    vec_out[...] = total
    turn(0)
    corner(0)
    finish(0)
    for g in range(GROUPS):
        for m in range(4):
            for core in range(2):
                put(g, m, core).wait()
        for k in range(1, shards):
            z_copy(g, k).wait_send()
        spread(g, quad, x_send.at[g], x_recv.at[g], x_peer).wait_send()
        spread(g, quad, y_send.at[g], y_recv.at[g], y_peer).wait_send()
        spread(g, y_quad, d_send.at[g, 0], d_recv.at[g, 0], x_peer, 0).wait_send()
        spread(g, x_quad, d_send.at[g, 1], d_recv.at[g, 1], y_peer, 1).wait_send()
        for i in range(4):
            spread(g, quad, g_send.at[g, i], g_recv.at[g, i], partner).wait_send()
    for m in range(4):
        cross(m).wait_send()
    for swap in swaps:
        swap.wait_send()
    save.wait()


def final_layer(shards, quads, dq, dk, dv, dkx, dvx, normed, x, attn, w_qkvo, d_out, up, down, vec, small):
    tokens, model = x.shape
    rows = model // shards // 2
    any_space = pl.BlockSpec(memory_space=pl.ANY)
    vmem_space = pl.BlockSpec(memory_space=pltpu.VMEM)
    dma = pltpu.SemaphoreType.DMA
    low, wide = jnp.bfloat16, jnp.float32
    piece = (rows, model)
    spare = max(quads - 1, 1)
    flat = pltpu.VMEM((tokens, model), low)
    return pl.pallas_call(
        functools.partial(final_body, shards, quads, rows),
        name="final_layer",
        out_shape=(
            jax.ShapeDtypeStruct((4, 2 * rows, model), low),
            jax.ShapeDtypeStruct((2 * rows, 4 * model), low),
            jax.ShapeDtypeStruct((8 * rows, model), low),
            jax.ShapeDtypeStruct(small.shape, wide),
            jax.ShapeDtypeStruct((tokens, model), low),
        ),
        in_specs=[any_space] * 10 + [vmem_space] * 4,
        out_specs=(any_space,) * 3 + (vmem_space, any_space),
        scratch_shapes=[flat] * 6
        + [pltpu.VMEM((model, tokens), low), flat, flat, pltpu.VMEM((3, model, model), low)]
        + [
            pltpu.VMEM((4, shards, 2) + piece, low),
            pltpu.VMEM((4, shards) + piece, low),
            pltpu.VMEM((shards, 2) + piece, low),
            pltpu.VMEM((shards,) + piece, low),
        ]
        + [pltpu.VMEM((shards - 1,) + piece, low)] * 3
        + [pltpu.VMEM((spare,) + piece, low)] * 3
        + [pltpu.VMEM((2, 4) + piece, low)] * 3
        + [
            pltpu.VMEM(small.shape, wide),
            pltpu.VMEM((2 + shards,) + small.shape, wide),
            pltpu.VMEM((quads,) + small.shape, wide),
            dma((10,)), dma((1,)), dma((2,)), dma((2,)),
            dma((4,)), dma((4,)),
            dma((shards, 2)), dma((shards, 2)),
            dma((shards,)), dma((shards,)),
            dma((GROUPS, shards - 1)), dma((GROUPS, shards - 1)),
            dma((GROUPS, spare)), dma((GROUPS, spare)),
            dma((GROUPS,)), dma((GROUPS,)), dma((GROUPS,)), dma((GROUPS,)),
            dma((GROUPS, 2)), dma((GROUPS, 2)),
            dma((GROUPS, 4)), dma((GROUPS, 4)),
            dma((GROUPS, 4, 2)),
            dma((3 + shards + quads,)), dma((3 + shards + quads,)),
        ],
        compiler_params=pltpu.CompilerParams(
            collective_id=1, has_side_effects=True, vmem_limit_bytes=62_000_000
        ),
    )(dq, dk, dv, dkx, dvx, normed, x, attn, w_qkvo, d_out, up, down, vec, small)


def on_device(
    shards, quads,
    layer_input, segment, rand_blocks, first_gain, first_bias, query_weight, query_bias,
    key_weight, value_weight, value_bias, out_weight, out_bias, second_gain, second_bias,
    up_weight, up_bias, down_weight, down_bias, cotangent,
):
    micro, _, half, model = layer_input.shape
    side = lax.axis_index("seq")
    rows = micro * half
    part = model // shards
    low, wide = jnp.bfloat16, jnp.float32
    shard = lax.axis_index("fsdp")
    vec = jnp.concatenate([
        first_gain, first_bias, query_bias, value_bias, out_bias, second_gain, second_bias, down_bias
    ]).reshape(8, part)
    vec = lax.dynamic_update_slice(jnp.zeros((16, model), low), vec, (0, shard * part))
    inside = lax.rem(shard * 4 * part, model)
    vec = lax.dynamic_update_slice(
        vec, up_bias.reshape(1, 4 * part), (8 + shard * 4 * part // model, inside)
    )
    w_qkvo, w_up, w_down, vec, normed, queries, keys, values, keys_other, values_other = gather_weights(
        shards, jnp.stack([query_weight, key_weight, value_weight, out_weight]), up_weight, down_weight, vec,
        layer_input.reshape(rows, model),
    )
    span, aug, block_bias, doc_bias = tables(segment[:, 0], rand_blocks[:, 0], side, half)

    cut = lambda array: array.reshape(micro, half, model)
    attended = (span, cut(queries), cut(keys), cut(values), cut(keys_other), cut(values_other),
                aug, block_bias, doc_bias)
    mixed, lse = attend_forward(*attended)
    mixed_rows = mixed.reshape(rows, model)
    tokens = layer_input.reshape(rows, model)
    result, grad_attn, grad_mixed, d_out, d_up, d_down, small = middle_layer(
        shards, mixed_rows, tokens, cotangent.reshape(rows, model), w_qkvo, w_up, w_down, vec
    )
    grads = attend_backward(0, (), *attended, mixed, cut(grad_mixed), lse)
    grads = attend_backward(1, grads, *attended, mixed, cut(grad_mixed), lse)
    grads = [array.reshape(rows, model) for array in (grads[0], grads[1], grads[2], grads[3], grads[4])]
    g_qkvo, g_up, g_down, small, input_grad = final_layer(
        shards, quads, *grads, normed, tokens, grad_attn, w_qkvo,
        d_out.reshape(shards, 2, part // 2, model), d_up, d_down, vec, small,
    )
    g_qkvo, g_up, g_down = g_qkvo.astype(wide), g_up.astype(wide), g_down.astype(wide)
    flat = lax.dynamic_slice(small, (0, shard * part), (8, part))
    d_b_up = lax.dynamic_slice(small, (8 + shard * 4 * part // model, inside), (1, 4 * part)).reshape(4 * part)
    shape = layer_input.shape
    return (
        result.reshape(shape), input_grad.reshape(shape), flat[4], flat[5], g_qkvo[0], flat[6],
        g_qkvo[1], g_qkvo[2], flat[7], g_qkvo[3], flat[2], flat[0], flat[1], g_up, d_b_up, g_down, flat[3],
    )


def solution(mesh):
    row = P(None, ("rep", "fsdp"), "seq", None)
    flat, wide = P("fsdp"), P("fsdp", None)
    shards, quads = mesh.shape["fsdp"], mesh.shape["rep"] // 4
    assert mesh.shape["seq"] == 2 and mesh.shape["rep"] % 4 == 0
    return jax.shard_map(
        functools.partial(on_device, shards, quads),
        mesh=mesh,
        in_specs=(
            row, P(None, ("rep", "fsdp"), None), P(None, ("rep", "fsdp"), None, None, None),
            flat, flat, wide, flat, wide, wide, flat, wide, flat, flat, flat, wide, flat, wide, flat, row,
        ),
        out_specs=(row, row, flat, flat, wide, flat, wide, wide, flat, wide, flat, flat, flat, wide, flat, wide, flat),
        check_vma=False,
    )
```

profile of v0, /device:TPU:25, one launch (start us, length us, event | category | flops | bytes accessed | tf_op | source)
XLA Modules:
  0.0 298.9 jit_solution(9198872052868474199)
XLA Ops:
  0.7 0.9 broadcast_add_fusion.1
  1.8 0.7 copy.100
  4.4 0.9 fusion.7.block_ref
  5.3 5.4 %concatenate.3 = bf16[1536]{0:T(1024)(128)(2,1)S(1)} concatenate(bf16[192]{0:T(256)(128)(2,1)} %param.22, bf16[192]{0:T(256)(128)(2,1)} %param.23, bf16[192]{0:T(256)(128)(2,1)} %param.25, bf16[192]{0:T(256)(128)(2,1)} %param.28, bf16[192]{0:T(256)(128)(2,1)} %param.30, bf16[192]{0:T(256)(128)(2,1)} %param.31, bf16[192]{0:T(256)(128)(2,1)} %param.32, bf16[192]{0:T(256)(128)(2,1)} %param.36), dimensions={0} | concatenate | bytes 6144 | tf_op jit(solution)/shard_map/concatenate | solution.py:1135
  11.5 0.7 reshape.447
  12.2 1.4 pad_maximum_fusion.qkvo_in
  13.6 71.8 %gather_weights.1 = (bf16[4,768,768]{2,1,0:T(8,128)(2,1)}, bf16[768,3072]{1,0:T(8,128)(2,1)}, bf16[3072,768]{1,0:T(8,128)(2,1)}, f32[16,768]{1,0:T(8,128)S(1)}, ...) custom-call(bf16[4,192,768]{2,1,0:T(8,128)(2,1)S(1)} %pad_maximum_fu, ...), custom_call_target="tpu_custom_call" | custom-call | tf_op jit(solution)/shard_map/gather_weights/pallas_call | solution.py:478
  85.4 1.1 copy-done.2
  87.1 1.0 fusion.3.doc_ref
  88.4 1.1 fusion.1.aug_ref
  89.5 20.0 %attend_forward.1 = (bf16[2,512,768]{2,1,0:T(8,128)(2,1)}, f32[2,6,2,512]{3,2,1,0:T(2,128)}) custom-call(s32[2,2,3]{2,1,0:T(2,128)} %add_add_fusion.span_ref, bf16[2,512,768]{2,1,0:T(8,128)(2,1)} %bitcast.95, bf16[2,512,768]{2,1,0:T(8,128)(2,1)} %bitcast.98, bf16[2,512,768]{2,1,0:T(8,128)(2,1)} %bitcast.101, bf16[2,512,768]{2,1,0:T(8,128)(2,1)} %bitcast.104, ...), custom_call_target="tpu_custom_call" | custom-call | flops 20000000000 | bytes 20000000 | tf_op jit(solution)/shard_map/attend_forward/pallas_call | solution.py:195
  109.5 70.7 %middle_layer.1 = (bf16[1024,768]{1,0:T(8,128)(2,1)}, bf16[1024,768]{1,0:T(8,128)(2,1)}, bf16[1024,768]{1,0:T(8,128)(2,1)}, bf16[768,768]{1,0:T(8,128)(2,1)}, bf...) custom-call(bf16[1024,768]{1,0:T(8,128)(2,1)} %bitcast.74, bf16[1024,768]{1,0:T(8,128)(2,1)} %bitcast.64, ...), custom_call_target="tpu_custom_call" | custom-call | tf_op jit(solution)/shard_map/middle_layer/pallas_call | solution.py:759
  180.2 15.7 %attend_backward.2 = (bf16[2,512,768]{2,1,0:T(8,128)(2,1)}, bf16[2,512,768]{2,1,0:T(8,128)(2,1)}, bf16[2,512,768]{2,1,0:T(8,128)(2,1)}, bf16[2,512,768]{2,1,0:T(8,128)(2,1)}, bf16[2,512,768]{2,1,0:T(8,128)(2,1)}) custom-call(s32[2,2,3]{2,1,0:T(2,128)} %add_add_fusion.span_ref, bf16[2,512,768]{2,1,0:T(8,128)(2,1)} %bitcast.96, bf16[2,512,768]{2,1,0:T(8,128)(2,1)} %bitcast.99, ...), custom_call_target="tpu_custom_call" | custom-call | flops 20000000000 | bytes 20000000 | tf_op jit(solution)/shard_map/attend_backward/pallas_call | solution.py:223
  195.9 20.0 %attend_backward.3 = (bf16[2,512,768]{2,1,0:T(8,128)(2,1)}, bf16[2,512,768]{2,1,0:T(8,128)(2,1)}, bf16[2,512,768]{2,1,0:T(8,128)(2,1)}, bf16[2,512,768]{2,1,0:T(8,128)(2,1)}, bf16[2,512,768]{2,1,0:T(8,128)(2,1)}) custom-call(s32[2,2,3]{2,1,0:T(2,128)} %add_add_fusion.span_ref, ...), custom_call_target="tpu_custom_call", output_to_operand_aliasing={{0}: (12, {}), {1}: (13, {}), {2}: (14, {}), {3}: (15, {}),... | custom-call | flops 20000000000 | bytes 20000000 | tf_op jit(solution)/shard_map/attend_backward/pallas_call | solution.py:223
  215.9 70.3 %final_layer.1 = (bf16[4,192,768]{2,1,0:T(8,128)(2,1)}, bf16[192,3072]{1,0:T(8,128)(2,1)}, bf16[768,768]{1,0:T(8,128)(2,1)}, f32[16,768]{1,0:T(8,128)}, bf16[1024,768]{1,0:T(8,128)(2,1)}) custom-call(bf16[1024,768]{1,0:T(8,128)(2,1)} %bitcast.66, bf16[1024,768]{1,0:T(8,128)(2,1)} %bitcast.67, bf16[1024,768]{1,0:T(8,128)(2,1)} %bitcast.68, ...), custom_call_target="tpu_custom_call" | custom-call | tf_op jit(solution)/shard_map/final_layer/pallas_call | solution.py:1078
  286.1 1.5 convert_element_type.21
  287.6 1.4 slice_bitcast_fusion
  289.6 1.7 convert_element_type.22
  291.2 1.6 convert_element_type.23
  292.8 1.3 dynamic-slice_reduce_fusion
  294.2 1.7 fusion.18
  295.8 1.1 copy.111
  297.0 0.8 copy-done.7
  297.8 1.1 copy.112
  (49 shorter events, 4.3 us)
Async XLA Ops:
  0.7 3.2 %copy-start = (s32[2,1,12,16,3]{3,1,4,2,0:T(1,128)S(1)}, s32[2,1,12,16,3]{3,1,4,2,0:T(1,128)}, u32[]{:S(2)}) copy-start(s32[2,1,12,16,3]{3,1,4,2,0:T(1,128)} %param.21) | copy-start | bytes 13828
  0.7 12.9 %copy-start.3 = (bf16[192,3072]{1,0:T(8,128)(2,1)S(1)}, bf16[192,3072]{1,0:T(8,128)(2,1)}, u32[]{:S(2)}) copy-start(bf16[192,3072]{1,0:T(8,128)(2,1)} %up_in.1) | copy-start | bytes 3538948
  0.7 12.9 %copy-start.4 = (bf16[768,768]{1,0:T(8,128)(2,1)S(1)}, bf16[768,768]{1,0:T(8,128)(2,1)}, u32[]{:S(2)}) copy-start(bf16[768,768]{1,0:T(8,128)(2,1)} %down_in.1) | copy-start | bytes 3538948
  13.6 74.8 %copy-start.10 = (s32[2,1,1024]{2,1,0:T(1,128)S(1)}, s32[2,1,1024]{2,1,0:T(1,128)}, u32[]{:S(2)}) copy-start(s32[2,1,1024]{2,1,0:T(1,128)} %param.20) | copy-start | bytes 24580
  85.4 1.1 copy-start.2
  86.5 0.6 copy-start.5
  287.6 2.0 copy-start.9
  289.6 1.7 copy-start.8
  291.2 4.6 %copy-start.6 = (bf16[1024,768]{1,0:T(8,128)(2,1)S(1)}, bf16[1024,768]{1,0:T(8,128)(2,1)}, u32[]{:S(2)}) copy-start(bf16[1024,768]{1,0:T(8,128)(2,1)} %get-tuple-element.61) | copy-start | bytes 4718596
  295.8 2.0 copy-start.7
  295.8 3.1 %copy-start.1 = (s32[2,1,12,16,3]{3,1,4,2,0:T(1,128)S(1)}, s32[2,1,12,16,3]{3,1,4,2,0:T(1,128)}, u32[]{:S(2)}) copy-start(s32[2,1,12,16,3]{3,1,4,2,0:T(1,128)} %param.21) | copy-start | bytes 13828
where the time goes:
time: 299 us
  Pallas kernels  268 us (90%)
  local copies, waits for them, and re-layouts  18.5 us (6%)
  other arithmetic  11.2 us (4%)
    pallas_call x1, Pallas kernels, gather_weights(): pl.pallas_call(functools.partial(gather_body, shards, rows), name='gather...  71.8 us
    pallas_call x1, Pallas kernels, middle_layer(): pl.pallas_call(functools.partial(middle_body, shards, rows), name='middle...  70.7 us
    pallas_call x1, Pallas kernels, final_layer(): pl.pallas_call(functools.partial(final_body, shards, quads, rows), name='...  70.3 us
    pallas_call x2, Pallas kernels, attend_backward(): pl.pallas_call(functools.partial(backward_body, step, len(carried)), name...  35.6 us
    pallas_call x1, Pallas kernels, attend_forward(): pl.pallas_call(forward_body, name='attend_forward', out_shape=(jax.ShapeD...  20 us
    unnamed x27, local copies, waits for them, and re-layouts  6.24 us

commit v1 on v0

--- a/solution.py
+++ b/solution.py
@@ -523,7 +523,7 @@
     mixed_in, x_in, grad_in, qkvo_in, up_w_in, down_w_in, vec_in,
     result_out, attn_out, mixed_out, d_out_out, up_out, down_out, sums_out,
     mixed, x, grad, out_w, up_w, down_w, middle, normed, turned, hidden, slope,
-    up_grad, down_grad, up_mate, down_mate, up_first, down_first, up_second, down_second,
+    up_grad, down_grad, up_mate, down_mate, up_first, down_first, down_second,
     load_sem, save_sem, uc_send, uc_recv, dc_send, dc_recv, f_send, f_recv, s_send, s_recv,
 ):
     rep, shard, side, quad, (dx, dy) = place()
@@ -543,7 +543,7 @@
     for load in loads:
         load.start()
     greet([(rep + dx, shard, side), (rep + dy, shard, side), partner])
-    firsts, seconds = (up_first, down_first), (up_second, down_second)
+    firsts = (up_first, down_first)
 
     def row(i):
         return vec_in[i:i + 1, :]
@@ -572,25 +572,31 @@
         member = quad + way if slot == 0 else quad + dx + dy
         return remote(part(g, f, member), firsts[g].at[f, slot], f_send.at[g, f, slot], f_recv.at[g, f, slot], (rep + way, shard, side))
 
-    def s_copy(g, f):
+    def s_copy(f):
         way = flip_way(f, 1)
-        return remote(part(g, f, quad + way), seconds[g].at[f], s_send.at[g, f], s_recv.at[g, f], (rep + way, shard, side))
-
-    def first_go(g, f):
-        for slot in range(2):
-            f_copy(g, f, slot).start()
+        return remote(part(1, f, quad + way), down_second.at[f], s_send.at[f], s_recv.at[f], (rep + way, shard, side))
+
+    def first_go(g, f, m):
+        @pl.when(m == quad + dx + dy)
+        def _():
+            f_copy(g, f, 1).start()
+
+        @pl.when(m == quad + flip_way(f, 0))
+        def _():
+            f_copy(g, f, 0).start()
 
     def down_merge(f):
         down_cross(f).wait_recv()
         for m in range(4):
             add_into(part(1, f, m), (part(1, f, m), mate(1, f, m)))
-        first_go(1, f)
+            first_go(1, f, m)
 
     def up_merge(m):
         up_cross(m).wait_recv()
 
         def step(f, carry):
             add_into(part(0, f, m), (part(0, f, m), mate(0, f, m)))
+            first_go(0, f, m)
             return carry
         lax.fori_loop(0, shards, step, 0)
 
@@ -600,20 +606,22 @@
             return carry
         lax.fori_loop(0, shards, step, 0)
 
-    def fold(g):
-        def body(f):
-            for slot in range(2):
-                f_copy(g, f, slot).wait()
-                member = quad if slot == 0 else quad + flip_way(f, 1)
-                add_into(part(g, f, member), (part(g, f, member), firsts[g].at[f, slot]))
-            s_copy(g, f).start()
-        each(body)
-
-    def settle(g, target):
-        def body(f):
-            s_copy(g, f).wait()
-            add_into(target.at[f], (part(g, f, quad), seconds[g].at[f]))
-        each(body)
+    def down_fold(f):
+        for slot in range(2):
+            f_copy(1, f, slot).wait()
+            member = quad if slot == 0 else quad + flip_way(f, 1)
+            add_into(part(1, f, member), (part(1, f, member), down_first.at[f, slot]))
+        s_copy(f).start()
+
+    def down_settle(f):
+        s_copy(f).wait()
+        add_into(down_out.at[f], (part(1, f, quad), down_second.at[f]))
+
+    def up_fold(f):
+        for slot in range(2):
+            f_copy(0, f, slot).wait()
+            member = quad if slot == 0 else quad + flip_way(f, 1)
+            add_into(up_out.at[slot, f], (part(0, f, member), up_first.at[f, slot]))
 
     saves = []
 
@@ -688,9 +696,8 @@
         contract(m)
         return carry
     lax.fori_loop(0, 4, contract_step, 0)
-    fold(1)
     up_merge(3)
-    each(lambda f: first_go(0, f))
+    each(down_fold)
 
     def finish(j, carry):
         at = block(j)
@@ -725,19 +732,17 @@
             attn_sum + column(attn.astype(wide)), grad_sum + column(upstream),
         )
     zero = jnp.zeros((1, model), wide)
-    sums = lax.fori_loop(0, steps // 2, back, (zero,) * 4)
-    fold(0)
-    sums = lax.fori_loop(steps // 2, steps, back, sums)
+    sums = lax.fori_loop(0, steps, back, (zero,) * 4)
     save(normed, mixed_out)
     save(grad, attn_out)
     for i, value in enumerate(sums):
         sums_out[i:i + 1, :] = value
     sums_out[4:8, :] = jnp.zeros((4, model), wide)
     sums_out[12:16, :] = jnp.zeros((4, model), wide)
-    settle(1, down_out)
+    each(down_settle)
     out_w[...] = tn(mixed[...], grad[...]).astype(low)
     save(out_w, d_out_out)
-    settle(0, up_out)
+    each(up_fold)
     for m in range(4):
         up_cross(m).wait_send()
     each(lambda f: down_cross(f).wait_send())
@@ -762,7 +767,7 @@
         out_shape=(
             token, token, token,
             jax.ShapeDtypeStruct((model, model), low),
-            jax.ShapeDtypeStruct((shards, rows, model), low),
+            jax.ShapeDtypeStruct((2, shards, rows, model), low),
             jax.ShapeDtypeStruct((shards, rows, model), low),
             jax.ShapeDtypeStruct((16, model), wide),
         ),
@@ -785,10 +790,9 @@
             pltpu.VMEM((shards, 2, rows, model), low),
             pltpu.VMEM((shards, 2, rows, model), low),
             pltpu.VMEM((shards, rows, model), low),
-            pltpu.VMEM((shards, rows, model), low),
             dma((4 + 2 * shards,)), dma((4,)),
             dma((4,)), dma((4,)), dma((shards,)), dma((shards,)),
-            dma((2, shards, 2)), dma((2, shards, 2)), dma((2, shards)), dma((2, shards)),
+            dma((2, shards, 2)), dma((2, shards, 2)), dma((shards,)), dma((shards,)),
         ],
         compiler_params=pltpu.CompilerParams(
             collective_id=2, has_side_effects=True, vmem_limit_bytes=66_000_000
@@ -800,9 +804,9 @@
     shards, quads, rows,
     dq_in, dk_in, dv_in, dkx_in, dvx_in, normed_in, x_in, attn_in, w_in, d_out_in, up_in, down_in, vec_in, small_in,
     qkvo_out, up_out, down_out, vec_out, input_out,
-    dq, dk, dv, dkx, dvx, normed, turned, x, attn, weights, grads, mate, first, second,
+    dq, dk, dv, dkx, dvx, normed, turned, x, attn, weights, grads, mate, first, second, up_sum, up_second,
     last, last_up, last_down, ring, ring_up, ring_down, full, full_up, full_down, vec_sum, vec_mate, vec_ring,
-    load_sem, save_sem, w_send, w_recv, c_send, c_recv, f_send, f_recv, s_send, s_recv, z_send, z_recv, q_send, q_recv,
+    load_sem, save_sem, w_send, w_recv, c_send, c_recv, f_send, f_recv, s_send, s_recv, z_send, z_recv, q_send, q_recv, u_send, u_recv,
     x_send, x_recv, y_send, y_recv, d_send, d_recv, g_send, g_recv, out_sem, v_send, v_recv,
 ):
     rep, shard, side, quad, (dx, dy) = place()
@@ -839,7 +843,7 @@
         return grads.at[m, f, side]
 
     def source(g, f):
-        return (part(f, quad), up_in.at[f], down_in.at[f])[g]
+        return (part(f, quad), up_sum.at[f], down_in.at[f])[g]
 
     def flip_way(f, after):
         odd = lax.rem(f + after, 2)
@@ -940,12 +944,22 @@
 
         def step(f, carry):
             add_into(part(f, m), (part(f, m), mate.at[m, f]))
+
+            @pl.when(m == d_quad)
+            def _():
+                f_copy(f, 1).start()
+
+            @pl.when(m == quad + flip_way(f, 0))
+            def _():
+                f_copy(f, 0).start()
             return carry
         lax.fori_loop(0, shards, step, 0)
 
-    for g in (2, 1):
-        for k in range(1, shards):
-            z_copy(g, k).start()
+    def u_copy(f):
+        return remote(up_in.at[1, f], up_second.at[f], u_send.at[f], u_recv.at[f], (rep + flip_way(f, 1), shard, side))
+    each(lambda f: u_copy(f).start())
+    for k in range(1, shards):
+        z_copy(2, k).start()
     loads[2].wait()
     cross(3).start()
     loads[0].wait()
@@ -969,10 +983,12 @@
         merge(i)
     merge(2)
 
-    def begin(f):
-        for slot in range(2):
-            f_copy(f, slot).start()
-    each(begin)
+    def up_settle(f):
+        u_copy(f).wait()
+        add_into(up_sum.at[f], (up_in.at[0, f], up_second.at[f]))
+    each(up_settle)
+    for k in range(1, shards):
+        z_copy(1, k).start()
     for load in loads[5:]:
         load.wait()
 
@@ -990,13 +1006,7 @@
         gain, bias, query, value = carry
         return gain + column(error * unit), bias + column(error), query + column(dq[at, :]), value + column(dv[at, :])
     zero = jnp.zeros((1, model), wide)
-    sums = lax.fori_loop(0, steps, back, (zero,) * 4)
-    save = pltpu.make_async_copy(x, input_out, save_sem.at[0])
-    save.start()
-    vec_sum[...] = small_in[...]
-    for i, value in enumerate(sums):
-        vec_sum[4 + i:5 + i, :] = value
-    vec_copy(vec_sum, 0, partner).start()
+    sums = lax.fori_loop(0, steps // 2, back, (zero,) * 4)
 
     def fold(f):
         for slot in range(2):
@@ -1005,11 +1015,13 @@
             add_into(part(f, member), (part(f, member), first.at[f, slot]))
         s_copy(f).start()
     each(fold)
-    vec_copy(vec_sum, 0, partner).wait()
-    vec_sum[...] = vec_sum[...] + vec_mate[0]
-    vec_copy(vec_sum, 1, x_peer).start()
-    swirl(2)
-    swirl(1)
+    sums = lax.fori_loop(steps // 2, steps, back, sums)
+    save = pltpu.make_async_copy(x, input_out, save_sem.at[0])
+    save.start()
+    vec_sum[...] = small_in[...]
+    for i, value in enumerate(sums):
+        vec_sum[4 + i:5 + i, :] = value
+    vec_copy(vec_sum, 0, partner).start()
 
     def settle(f):
         s_copy(f).wait()
@@ -1017,6 +1029,11 @@
     each(settle)
     for k in range(1, shards):
         z_copy(0, k).start()
+    vec_copy(vec_sum, 0, partner).wait()
+    vec_sum[...] = vec_sum[...] + vec_mate[0]
+    vec_copy(vec_sum, 1, x_peer).start()
+    swirl(2)
+    swirl(1)
     vec_copy(vec_sum, 1, x_peer).wait()
     vec_sum[...] = vec_sum[...] + vec_mate[1]
     vec_copy(vec_sum, 2, y_peer).start()
@@ -1094,6 +1111,8 @@
             pltpu.VMEM((4, shards) + piece, low),
             pltpu.VMEM((shards, 2) + piece, low),
             pltpu.VMEM((shards,) + piece, low),
+            pltpu.VMEM((shards,) + piece, low),
+            pltpu.VMEM((shards,) + piece, low),
         ]
         + [pltpu.VMEM((shards - 1,) + piece, low)] * 3
         + [pltpu.VMEM((spare,) + piece, low)] * 3
@@ -1107,7 +1126,7 @@
             dma((shards, 2)), dma((shards, 2)),
             dma((shards,)), dma((shards,)),
             dma((GROUPS, shards - 1)), dma((GROUPS, shards - 1)),
-            dma((GROUPS, spare)), dma((GROUPS, spare)),
+            dma((GROUPS, spare)), dma((GROUPS, spare)), dma((shards,)), dma((shards,)),
             dma((GROUPS,)), dma((GROUPS,)), dma((GROUPS,)), dma((GROUPS,)),
             dma((GROUPS, 2)), dma((GROUPS, 2)),
             dma((GROUPS, 4)), dma((GROUPS, 4)),
@@ -1132,14 +1151,17 @@
     part = model // shards
     low, wide = jnp.bfloat16, jnp.float32
     shard = lax.axis_index("fsdp")
-    vec = jnp.concatenate([
-        first_gain, first_bias, query_bias, value_bias, out_bias, second_gain, second_bias, down_bias
-    ]).reshape(8, part)
+    rank = lax.broadcasted_iota(jnp.int32, (16, 1), 0)
+    vec = jnp.zeros((16, part), low)
+    for i, bias in enumerate((first_gain, first_bias, query_bias, value_bias, out_bias, second_gain, second_bias, down_bias)):
+        vec = jnp.where(rank == i, bias[None, :], vec)
     vec = lax.dynamic_update_slice(jnp.zeros((16, model), low), vec, (0, shard * part))
     inside = lax.rem(shard * 4 * part, model)
-    vec = lax.dynamic_update_slice(
-        vec, up_bias.reshape(1, 4 * part), (8 + shard * 4 * part // model, inside)
-    )
+    line = 8 + shard * 4 * part // model
+    if 4 * part == model:
+        vec = jnp.where(rank == line, up_bias[None, :], vec)
+    else:
+        vec = lax.dynamic_update_slice(vec, up_bias.reshape(1, 4 * part), (line, inside))
     w_qkvo, w_up, w_down, vec, normed, queries, keys, values, keys_other, values_other = gather_weights(
         shards, jnp.stack([query_weight, key_weight, value_weight, out_weight]), up_weight, down_weight, vec,
         layer_input.reshape(rows, model),
@@ -1164,7 +1186,7 @@
     )
     g_qkvo, g_up, g_down = g_qkvo.astype(wide), g_up.astype(wide), g_down.astype(wide)
     flat = lax.dynamic_slice(small, (0, shard * part), (8, part))
-    d_b_up = lax.dynamic_slice(small, (8 + shard * 4 * part // model, inside), (1, 4 * part)).reshape(4 * part)
+    d_b_up = lax.dynamic_slice(small, (line, inside), (1, 4 * part)).reshape(4 * part)
     shape = layer_input.shape
     return (
         result.reshape(shape), input_grad.reshape(shape), flat[4], flat[5], g_qkvo[0], flat[6],

time: 299 us -> 285 us (0.953); the launches traced: 299 us -> 280 us
  Pallas kernels: 268 us -> 254 us
  local copies, waits for them, and re-layouts: 18.5 us -> 12.2 us
    pallas_call x1, Pallas kernels: 70.7 us -> 62.1 us  [middle_layer(): pl.pallas_call(functools.partial(middle_body, shards, rows), name='middle...]
    concatenate x1 -> x0, local copies, waits for them, and re-layouts: 5.42 us -> none  [on_device(): jnp.concatenate([first_gain, first_bias, query_bias, value_bias, out_bias...]
    pallas_call x2, Pallas kernels: 35.6 us -> 31.4 us  [attend_backward(): pl.pallas_call(functools.partial(backward_body, step, len(carried)), name...]
where the time goes in v1:
time: 285 us; the launch traced here: 280 us
  Pallas kernels  254 us (89%)
  other arithmetic  12.7 us (4%)
  local copies, waits for them, and re-layouts  12.2 us (4%)
    pallas_call x1, Pallas kernels, gather_weights(): pl.pallas_call(functools.partial(gather_body, shards, rows), name='gather...  71.8 us
    pallas_call x1, Pallas kernels, final_layer(): pl.pallas_call(functools.partial(final_body, shards, quads, rows), name='...  71.5 us
    pallas_call x1, Pallas kernels, middle_layer(): pl.pallas_call(functools.partial(middle_body, shards, rows), name='middle...  62.1 us
    pallas_call x2, Pallas kernels, attend_backward(): pl.pallas_call(functools.partial(backward_body, step, len(carried)), name...  31.4 us
    pallas_call x1, Pallas kernels, attend_forward(): pl.pallas_call(forward_body, name='attend_forward', out_shape=(jax.ShapeD...  17.3 us
    unnamed x27, local copies, waits for them, and re-layouts  6.39 us

profile of v1, /device:TPU:25, one launch (start us, length us, event | category | flops | bytes accessed | tf_op | source)
XLA Modules:
  0.0 279.9 jit_solution(5602469629362900234)
XLA Ops:
  0.7 0.7 broadcast_add_fusion.1
  1.6 0.9 copy.100
  4.4 0.9 fusion.7.block_ref
  5.3 0.9 select_select_fusion
  6.6 0.8 broadcast_select_fusion.vec_in
  7.4 1.4 pad_maximum_fusion.qkvo_in
  8.8 71.8 %gather_weights.1 = (bf16[4,768,768]{2,1,0:T(8,128)(2,1)}, bf16[768,3072]{1,0:T(8,128)(2,1)}, bf16[3072,768]{1,0:T(8,128)(2,1)}, f32[16,768]{1,0:T(8,128)S(1)}, ...) custom-call(bf16[4,192,768]{2,1,0:T(8,128)(2,1)S(1)} %pad_maximum_fu, ...), custom_call_target="tpu_custom_call" | custom-call | tf_op jit(solution)/shard_map/gather_weights/pallas_call | solution.py:478
  80.6 1.1 copy-done.2
  82.3 1.0 fusion.3.doc_ref
  83.6 1.1 fusion.1.aug_ref
  84.7 17.3 %attend_forward.1 = (bf16[2,512,768]{2,1,0:T(8,128)(2,1)}, f32[2,6,2,512]{3,2,1,0:T(2,128)}) custom-call(s32[2,2,3]{2,1,0:T(2,128)} %add_add_fusion.span_ref, bf16[2,512,768]{2,1,0:T(8,128)(2,1)} %bitcast.95, bf16[2,512,768]{2,1,0:T(8,128)(2,1)} %bitcast.98, bf16[2,512,768]{2,1,0:T(8,128)(2,1)} %bitcast.101, bf16[2,512,768]{2,1,0:T(8,128)(2,1)} %bitcast.104, ...), custom_call_target="tpu_custom_call" | custom-call | flops 20000000000 | bytes 20000000 | tf_op jit(solution)/shard_map/attend_forward/pallas_call | solution.py:195
  102.0 62.1 %middle_layer.1 = (bf16[1024,768]{1,0:T(8,128)(2,1)}, bf16[1024,768]{1,0:T(8,128)(2,1)}, bf16[1024,768]{1,0:T(8,128)(2,1)}, bf16[768,768]{1,0:T(8,128)(2,1)}, bf...) custom-call(bf16[1024,768]{1,0:T(8,128)(2,1)} %bitcast.74, ...), custom_call_target="tpu_custom_call" | custom-call | tf_op jit(solution)/shard_map/middle_layer/pallas_call | solution.py:764
  164.1 15.7 %attend_backward.2 = (bf16[2,512,768]{2,1,0:T(8,128)(2,1)}, bf16[2,512,768]{2,1,0:T(8,128)(2,1)}, bf16[2,512,768]{2,1,0:T(8,128)(2,1)}, bf16[2,512,768]{2,1,0:T(8,128)(2,1)}, bf16[2,512,768]{2,1,0:T(8,128)(2,1)}) custom-call(s32[2,2,3]{2,1,0:T(2,128)} %add_add_fusion.span_ref, bf16[2,512,768]{2,1,0:T(8,128)(2,1)} %bitcast.96, bf16[2,512,768]{2,1,0:T(8,128)(2,1)} %bitcast.99, ...), custom_call_target="tpu_custom_call" | custom-call | flops 20000000000 | bytes 20000000 | tf_op jit(solution)/shard_map/attend_backward/pallas_call | solution.py:223
  179.8 15.7 %attend_backward.3 = (bf16[2,512,768]{2,1,0:T(8,128)(2,1)}, bf16[2,512,768]{2,1,0:T(8,128)(2,1)}, bf16[2,512,768]{2,1,0:T(8,128)(2,1)}, bf16[2,512,768]{2,1,0:T(8,128)(2,1)}, bf16[2,512,768]{2,1,0:T(8,128)(2,1)}) custom-call(s32[2,2,3]{2,1,0:T(2,128)} %add_add_fusion.span_ref, ...), custom_call_target="tpu_custom_call", output_to_operand_aliasing={{0}: (12, {}), {1}: (13, {}), {2}: (14, {}), {3}: (15, {}),... | custom-call | flops 20000000000 | bytes 20000000 | tf_op jit(solution)/shard_map/attend_backward/pallas_call | solution.py:223
  195.5 71.5 %final_layer.1 = (bf16[4,192,768]{2,1,0:T(8,128)(2,1)}, bf16[192,3072]{1,0:T(8,128)(2,1)}, bf16[768,768]{1,0:T(8,128)(2,1)}, f32[16,768]{1,0:T(8,128)}, bf16[1024,768]{1,0:T(8,128)(2,1)}) custom-call(bf16[1024,768]{1,0:T(8,128)(2,1)} %bitcast.66, bf16[1024,768]{1,0:T(8,128)(2,1)} %bitcast.67, bf16[1024,768]{1,0:T(8,128)(2,1)} %bitcast.68, ...), custom_call_target="tpu_custom_call" | custom-call | tf_op jit(solution)/shard_map/final_layer/pallas_call | solution.py:1095
  267.0 1.5 convert_element_type.21
  268.5 1.4 slice_bitcast_fusion
  270.5 1.7 convert_element_type.22
  272.2 1.6 convert_element_type.23
  273.7 1.3 dynamic-slice_reduce_fusion
  275.1 1.7 fusion.18
  276.8 1.1 copy.110
  277.9 0.8 copy-done.7
  278.7 1.1 copy.111
  (52 shorter events, 3.9 us)
Async XLA Ops:
  0.7 3.2 %copy-start = (s32[2,1,12,16,3]{3,1,4,2,0:T(1,128)S(1)}, s32[2,1,12,16,3]{3,1,4,2,0:T(1,128)}, u32[]{:S(2)}) copy-start(s32[2,1,12,16,3]{3,1,4,2,0:T(1,128)} %param.21) | copy-start | bytes 13828
  1.6 7.1 %copy-start.3 = (bf16[192,3072]{1,0:T(8,128)(2,1)S(1)}, bf16[192,3072]{1,0:T(8,128)(2,1)}, u32[]{:S(2)}) copy-start(bf16[192,3072]{1,0:T(8,128)(2,1)} %up_in.1) | copy-start | bytes 3538948
  1.6 7.1 %copy-start.4 = (bf16[768,768]{1,0:T(8,128)(2,1)S(1)}, bf16[768,768]{1,0:T(8,128)(2,1)}, u32[]{:S(2)}) copy-start(bf16[768,768]{1,0:T(8,128)(2,1)} %down_in.1) | copy-start | bytes 3538948
  8.8 74.8 %copy-start.10 = (s32[2,1,1024]{2,1,0:T(1,128)S(1)}, s32[2,1,1024]{2,1,0:T(1,128)}, u32[]{:S(2)}) copy-start(s32[2,1,1024]{2,1,0:T(1,128)} %param.20) | copy-start | bytes 24580
  80.6 1.1 copy-start.2
  81.7 0.6 copy-start.5
  268.5 2.0 copy-start.9
  270.5 1.7 copy-start.8
  272.2 4.6 %copy-start.6 = (bf16[1024,768]{1,0:T(8,128)(2,1)S(1)}, bf16[1024,768]{1,0:T(8,128)(2,1)}, u32[]{:S(2)}) copy-start(bf16[1024,768]{1,0:T(8,128)(2,1)} %get-tuple-element.61) | copy-start | bytes 4718596
  276.7 2.0 copy-start.7
  276.8 3.1 %copy-start.1 = (s32[2,1,12,16,3]{3,1,4,2,0:T(1,128)S(1)}, s32[2,1,12,16,3]{3,1,4,2,0:T(1,128)}, u32[]{:S(2)}) copy-start(s32[2,1,12,16,3]{3,1,4,2,0:T(1,128)} %param.21) | copy-start | bytes 13828

commit v2 on v1

--- a/solution.py
+++ b/solution.py
@@ -290,11 +290,8 @@
     low = side * rows
     if group == 0:
         return refs[0].at[quad, pl.ds(pl.multiple_of(shard * (2 * rows) + low, 16), rows), pl.ds(offset, width)]
-    if group == 1:
-        at = pl.multiple_of(shard * (2 * rows) + low, 16)
-        return refs[1].at[pl.ds(at, rows), pl.ds(pl.multiple_of(quad * 768 + offset, 128), width)]
-    at = pl.multiple_of(shard * (8 * rows) + quad * (2 * rows) + low, 16)
-    return refs[2].at[pl.ds(at, rows), pl.ds(offset, width)]
+    at = pl.multiple_of(shard * (2 * rows) + low, 16)
+    return refs[1].at[pl.ds(at, rows), pl.ds(pl.multiple_of(quad * 768 + offset, 128), width)]
 
 
 def greet(peers):
@@ -313,13 +310,13 @@
 def gather_body(
     shards, rows, qkvo_in, up_in, down_in, vec_in, x_in,
     qkvo_out, up_out, down_out, vec_out, normed_out, q_out, k_out, v_out, kx_out, vx_out,
-    qkvo_stage, up_stage, down_stage, vec_all, weights, normed, results,
+    qkvo_stage, up_stage, vec_all, weights, normed, results,
     in_sem, out_sem, z_send, z_recv, x_send, x_recv, y_send, y_recv, d_send, d_recv, c_send, c_recv,
     load_sem, save_sem, swap_send, swap_recv,
 ):
     rep, shard, side, quad, (dx, dy) = place()
-    ins, outs = (qkvo_in, up_in, down_in), (qkvo_out, up_out, down_out)
-    stages = (qkvo_stage, up_stage, down_stage)
+    ins, outs = (qkvo_in, up_in), (qkvo_out, up_out)
+    stages = (qkvo_stage, up_stage)
     x_peer, y_peer, partner = (rep + dx, shard, side), (rep + dy, shard, side), (rep, shard, 1 - side)
     z_peers = [(rep, lax.rem(shard + k, shards), side) for k in range(1, shards)]
     for i, src in enumerate(ins):
@@ -331,7 +328,7 @@
         copy.start()
         sent.append(copy)
 
-    for g in range(GROUPS):
+    for g in range(EARLY):
         for k in range(1, shards):
             go(remote(
                 chunk(ins, g, 0, quad, side, rows), chunk(outs, g, shard, quad, side, rows),
@@ -341,12 +338,16 @@
             for k in range(1, shards):
                 go(remote(
                     vec_in, vec_all.at[k - 1],
-                    z_send.at[GROUPS, k - 1], z_recv.at[GROUPS, k - 1], z_peers[k - 1],
+                    z_send.at[EARLY, k - 1], z_recv.at[EARLY, k - 1], z_peers[k - 1],
                 ))
+    for k in range(1, shards):
+        go(remote(
+            down_in.at[pl.ds(pl.multiple_of((quad * 2 + side) * rows, 16), rows), :], down_out.at[shard],
+            z_send.at[EARLY + 1, k - 1], z_recv.at[EARLY + 1, shards - k - 1], z_peers[k - 1],
+        ))
     owned = (
         qkvo_out.at[:, pl.ds(pl.multiple_of(shard * 2 * rows, 16), 2 * rows), :],
         up_out.at[pl.ds(pl.multiple_of(shard * 2 * rows, 16), 2 * rows), :],
-        down_out.at[pl.ds(pl.multiple_of(shard * 8 * rows, 16), 8 * rows), :],
     )
     local = []
     for i, src in enumerate(ins):
@@ -424,7 +425,7 @@
     straight(0)
     for k in range(1, shards):
         remote(
-            vec_in, vec_all.at[k - 1], z_send.at[GROUPS, k - 1], z_recv.at[GROUPS, k - 1], z_peers[k - 1]
+            vec_in, vec_all.at[k - 1], z_send.at[EARLY, k - 1], z_recv.at[EARLY, k - 1], z_peers[k - 1]
         ).wait_recv()
     total = vec_in[...].astype(jnp.float32)
     for k in range(1, shards):
@@ -436,25 +437,26 @@
     save(3, normed_out)
     straight(1)
     corner(0)
-    turn(1)
     local[0].wait()
     gathered(0)
     for i in (1, 2, 0):
         pltpu.make_async_copy(qkvo_out.at[i], weights.at[i], load_sem.at[i]).start()
-    straight(2)
     project(1, None)
     keys = exchange(1, kx_out)
     save(1, k_out)
-    corner(1)
+    turn(1)
     project(2, 3)
     values = exchange(2, vx_out)
     save(2, v_out)
-    turn(2)
+    corner(1)
     project(0, 2)
     save(0, q_out)
-    corner(2)
     gathered(1)
-    gathered(2)
+    for k in range(1, shards):
+        remote(
+            down_out.at[shard], down_out.at[lax.rem(shard + k, shards)],
+            z_send.at[EARLY + 1, k - 1], z_recv.at[EARLY + 1, k - 1], z_peers[k - 1],
+        ).wait_recv()
     keys.wait()
     values.wait()
     for copy in sent:
@@ -464,6 +466,7 @@
 
 
 STEP = 256
+EARLY = 2
 
 
 def gather_weights(shards, qkvo, up, down, vec, x):
@@ -481,24 +484,24 @@
         out_shape=(
             jax.ShapeDtypeStruct((4, model, model), low),
             jax.ShapeDtypeStruct((model, hidden), low),
-            jax.ShapeDtypeStruct((hidden, model), low),
+            jax.ShapeDtypeStruct((shards, rows, model), low),
             jax.ShapeDtypeStruct(vec.shape, jnp.float32),
         )
         + (token,) * 6,
         in_specs=[any_space] * 3 + [vmem_space] * 2,
         out_specs=(any_space,) * 3 + (vmem_space,) + (any_space,) * 6,
         scratch_shapes=[
-            pltpu.VMEM(qkvo.shape, low), pltpu.VMEM(up.shape, low), pltpu.VMEM(down.shape, low),
+            pltpu.VMEM(qkvo.shape, low), pltpu.VMEM(up.shape, low),
             pltpu.VMEM((shards - 1,) + vec.shape, low),
             pltpu.VMEM((3, model, model), low),
             pltpu.VMEM(x.shape, low),
             pltpu.VMEM((3,) + x.shape, low),
-            dma((3,)), dma((3,)),
-            dma((GROUPS + 1, shards - 1)), dma((GROUPS + 1, shards - 1)),
+            dma((2,)), dma((2,)),
+            dma((EARLY + 2, shards - 1)), dma((EARLY + 2, shards - 1)),
         ]
-        + [dma((GROUPS, shards - 1))] * 4
-        + [dma((GROUPS, shards - 1, 2))] * 2
-        + [dma((GROUPS, shards - 1, 4))] * 2
+        + [dma((EARLY, shards - 1))] * 4
+        + [dma((EARLY, shards - 1, 2))] * 2
+        + [dma((EARLY, shards - 1, 4))] * 2
         + [dma((3,)), dma((4,)), dma((2,)), dma((2,))],
         compiler_params=pltpu.CompilerParams(
             collective_id=0, has_side_effects=True, vmem_limit_bytes=50_000_000
@@ -520,11 +523,12 @@
 
 def middle_body(
     shards, rows,
-    mixed_in, x_in, grad_in, qkvo_in, up_w_in, down_w_in, vec_in,
+    mixed_in, x_in, grad_in, qkvo_in, up_w_in, down_w_in, down_z_in, vec_in,
     result_out, attn_out, mixed_out, d_out_out, up_out, down_out, sums_out,
     mixed, x, grad, out_w, up_w, down_w, middle, normed, turned, hidden, slope,
     up_grad, down_grad, up_mate, down_mate, up_first, down_first, down_second,
     load_sem, save_sem, uc_send, uc_recv, dc_send, dc_recv, f_send, f_recv, s_send, s_recv,
+    x_send, x_recv, y_send, y_recv, d_send, d_recv, g_send, g_recv,
 ):
     rep, shard, side, quad, (dx, dy) = place()
     partner = (rep, shard, 1 - side)
@@ -539,10 +543,70 @@
     for f in range(shards):
         at = pl.ds(f * width, width)
         loads.append(pltpu.make_async_copy(up_w_in.at[:, at], up_w.at[f], load_sem.at[4 + f]))
-        loads.append(pltpu.make_async_copy(down_w_in.at[at, :], down_w.at[f], load_sem.at[4 + shards + f]))
+    loads.append(pltpu.make_async_copy(down_w_in, down_w.at[shard], load_sem.at[4 + shards]))
+    for k in range(1, shards):
+        f = lax.rem(shard + k, shards)
+        at = pl.ds(pl.multiple_of((quad * 2 + side) * rows, 16), rows)
+        loads.append(pltpu.make_async_copy(down_z_in.at[f], down_w.at[f, at, :], load_sem.at[4 + shards + k]))
     for load in loads:
         load.start()
-    greet([(rep + dx, shard, side), (rep + dy, shard, side), partner])
+    x_peer, y_peer = (rep + dx, shard, side), (rep + dy, shard, side)
+    x_quad, y_quad, d_quad = quad + dx, quad + dy, quad + dx + dy
+    greet([x_peer, y_peer, partner])
+
+    def piece(f, member, core, half=None):
+        at = pl.ds(pl.multiple_of((member * 2 + core) * rows, 16), rows)
+        if half is None:
+            return down_w.at[f, at, :]
+        return down_w.at[f, at, pl.ds(half * (model // 2), model // 2)]
+
+    def hop(k, member, core, send, recv, peer, half=None):
+        ref = piece(lax.rem(shard + k, shards), member, core, half)
+        return remote(ref, ref, send, recv, peer)
+
+    def own_piece(k, send, recv, peer):
+        f = lax.rem(shard + k, shards)
+        return remote(down_z_in.at[f], piece(f, quad, side), send, recv, peer)
+
+    def straight(k):
+        return (
+            own_piece(k, x_send.at[k - 1], x_recv.at[k - 1], x_peer),
+            own_piece(k, y_send.at[k - 1], y_recv.at[k - 1], y_peer),
+            own_piece(k, g_send.at[k - 1, 0], g_recv.at[k - 1, 0], partner),
+        )
+
+    def turn():
+        for k in range(1, shards):
+            hop(k, x_quad, side, x_send.at[k - 1], x_recv.at[k - 1], x_peer).wait_recv()
+            hop(k, x_quad, side, d_send.at[k - 1, 1], d_recv.at[k - 1, 1], y_peer, 1).start()
+            hop(k, x_quad, side, g_send.at[k - 1, 1], g_recv.at[k - 1, 1], partner).start()
+            hop(k, y_quad, side, y_send.at[k - 1], y_recv.at[k - 1], y_peer).wait_recv()
+            hop(k, y_quad, side, d_send.at[k - 1, 0], d_recv.at[k - 1, 0], x_peer, 0).start()
+            hop(k, y_quad, side, g_send.at[k - 1, 2], g_recv.at[k - 1, 2], partner).start()
+
+    def corner():
+        for k in range(1, shards):
+            hop(k, d_quad, side, d_send.at[k - 1, 0], d_recv.at[k - 1, 0], x_peer, 0).wait_recv()
+            hop(k, d_quad, side, d_send.at[k - 1, 1], d_recv.at[k - 1, 1], y_peer, 1).wait_recv()
+            hop(k, d_quad, side, g_send.at[k - 1, 3], g_recv.at[k - 1, 3], partner).start()
+
+    def gathered():
+        for k in range(1, shards):
+            for i, member in enumerate((quad, x_quad, y_quad, d_quad)):
+                hop(k, member, 1 - side, g_send.at[k - 1, i], g_recv.at[k - 1, i], partner).wait_recv()
+
+    def flushed():
+        for k in range(1, shards):
+            for copy in straight(k):
+                copy.wait_send()
+            hop(k, y_quad, side, d_send.at[k - 1, 0], d_recv.at[k - 1, 0], x_peer, 0).wait_send()
+            hop(k, x_quad, side, d_send.at[k - 1, 1], d_recv.at[k - 1, 1], y_peer, 1).wait_send()
+            for i in range(1, 4):
+                hop(k, quad, side, g_send.at[k - 1, i], g_recv.at[k - 1, i], partner).wait_send()
+
+    for k in range(1, shards):
+        for copy in straight(k):
+            copy.start()
     firsts = (up_first, down_first)
 
     def row(i):
@@ -668,7 +732,16 @@
         @pl.when(f > 0)
         def _():
             down_merge(f - 1)
+
+        @pl.when(f == 0)
+        def _():
+            turn()
+
+        @pl.when(f == 1)
+        def _():
+            corner()
     each(expand)
+    gathered()
 
     def contract(m):
         for h in range(model // width):
@@ -746,11 +819,12 @@
     for m in range(4):
         up_cross(m).wait_send()
     each(lambda f: down_cross(f).wait_send())
+    flushed()
     for copy in saves:
         copy.wait()
 
 
-def middle_layer(shards, mixed, x, grad, qkvo, up_w, down_w, vec):
+def middle_layer(shards, mixed, x, grad, qkvo, up_w, down_w, down_z, vec):
     tokens, model = x.shape
     hidden = up_w.shape[1]
     rows = model // shards // 2
@@ -771,7 +845,7 @@
             jax.ShapeDtypeStruct((shards, rows, model), low),
             jax.ShapeDtypeStruct((16, model), wide),
         ),
-        in_specs=[any_space] * 6 + [vmem_space],
+        in_specs=[any_space] * 7 + [vmem_space],
         out_specs=(any_space,) * 4 + (vmem_space,) * 3,
         scratch_shapes=[
             flat, flat, flat,
@@ -793,11 +867,14 @@
             dma((4 + 2 * shards,)), dma((4,)),
             dma((4,)), dma((4,)), dma((shards,)), dma((shards,)),
             dma((2, shards, 2)), dma((2, shards, 2)), dma((shards,)), dma((shards,)),
-        ],
+        ]
+        + [dma((shards - 1,))] * 4
+        + [dma((shards - 1, 2))] * 2
+        + [dma((shards - 1, 4))] * 2,
         compiler_params=pltpu.CompilerParams(
             collective_id=2, has_side_effects=True, vmem_limit_bytes=66_000_000
         ),
-    )(mixed, x, grad, qkvo, up_w, down_w, vec)
+    )(mixed, x, grad, qkvo, up_w, down_w, down_z, vec)
 
 
 def final_body(
@@ -1162,7 +1239,7 @@
         vec = jnp.where(rank == line, up_bias[None, :], vec)
     else:
         vec = lax.dynamic_update_slice(vec, up_bias.reshape(1, 4 * part), (line, inside))
-    w_qkvo, w_up, w_down, vec, normed, queries, keys, values, keys_other, values_other = gather_weights(
+    w_qkvo, w_up, down_z, vec, normed, queries, keys, values, keys_other, values_other = gather_weights(
         shards, jnp.stack([query_weight, key_weight, value_weight, out_weight]), up_weight, down_weight, vec,
         layer_input.reshape(rows, model),
     )
@@ -1175,7 +1252,7 @@
     mixed_rows = mixed.reshape(rows, model)
     tokens = layer_input.reshape(rows, model)
     result, grad_attn, grad_mixed, d_out, d_up, d_down, small = middle_layer(
-        shards, mixed_rows, tokens, cotangent.reshape(rows, model), w_qkvo, w_up, w_down, vec
+        shards, mixed_rows, tokens, cotangent.reshape(rows, model), w_qkvo, w_up, down_weight, down_z, vec
     )
     grads = attend_backward(0, (), *attended, mixed, cut(grad_mixed), lse)
     grads = attend_backward(1, grads, *attended, mixed, cut(grad_mixed), lse)

time: 285 us -> 278 us (0.975); the launches traced: 280 us -> 278 us
  Pallas kernels: 254 us -> 251 us
    pallas_call x1, Pallas kernels: 71.8 us -> 56.9 us  [gather_weights(): pl.pallas_call(functools.partial(gather_body, shards, rows), name='gather...]
    pallas_call x2, Pallas kernels: 31.4 us -> 35.4 us  [attend_backward(): pl.pallas_call(functools.partial(backward_body, step, len(carried)), name...]
where the time goes in v2:
time: 278 us
  Pallas kernels  251 us (90%)
  local copies, waits for them, and re-layouts  13 us (5%)
  other arithmetic  12.7 us (5%)
    pallas_call x1, Pallas kernels, final_layer(): pl.pallas_call(functools.partial(final_body, shards, quads, rows), name='...  73.7 us
    pallas_call x1, Pallas kernels, middle_layer(): pl.pallas_call(functools.partial(middle_body, shards, rows), name='middle...  64.9 us
    pallas_call x1, Pallas kernels, gather_weights(): pl.pallas_call(functools.partial(gather_body, shards, rows), name='gather...  56.9 us
    pallas_call x2, Pallas kernels, attend_backward(): pl.pallas_call(functools.partial(backward_body, step, len(carried)), name...  35.4 us
    pallas_call x1, Pallas kernels, attend_forward(): pl.pallas_call(forward_body, name='attend_forward', out_shape=(jax.ShapeD...  20 us
    unnamed x27, local copies, waits for them, and re-layouts  7.23 us

profile of v2, /device:TPU:25, one launch (start us, length us, event | category | flops | bytes accessed | tf_op | source)
XLA Modules:
  0.0 277.6 jit_solution(3258581501803579334)
XLA Ops:
  1.6 0.9 copy.100
  4.4 0.9 fusion.7.block_ref
  5.3 0.9 select_select_fusion
  6.6 0.8 broadcast_select_fusion.vec_in
  7.4 1.4 pad_maximum_fusion.qkvo_in
  8.8 56.9 %gather_weights.1 = (bf16[4,768,768]{2,1,0:T(8,128)(2,1)}, bf16[768,3072]{1,0:T(8,128)(2,1)}, bf16[4,96,768]{2,1,0:T(8,128)(2,1)S(1)}, f32[16,768]{1,0:T(8,128)S...) custom-call(bf16[4,192,768]{2,1,0:T(8,128)(2,1)S(1)} %pad_maximum_fu, ...), custom_call_target="tpu_custom_call" | custom-call | tf_op jit(solution)/shard_map/gather_weights/pallas_call | solution.py:481
  65.7 1.2 copy-done.2
  66.8 0.8 copy-done.4
  68.3 1.0 fusion.3.doc_ref
  69.5 1.1 fusion.1.aug_ref
  70.7 20.0 %attend_forward.1 = (bf16[2,512,768]{2,1,0:T(8,128)(2,1)}, f32[2,6,2,512]{3,2,1,0:T(2,128)}) custom-call(s32[2,2,3]{2,1,0:T(2,128)} %add_add_fusion.span_ref, bf16[2,512,768]{2,1,0:T(8,128)(2,1)} %bitcast.95, bf16[2,512,768]{2,1,0:T(8,128)(2,1)} %bitcast.98, bf16[2,512,768]{2,1,0:T(8,128)(2,1)} %bitcast.101, bf16[2,512,768]{2,1,0:T(8,128)(2,1)} %bitcast.104, ...), custom_call_target="tpu_custom_call" | custom-call | flops 20000000000 | bytes 20000000 | tf_op jit(solution)/shard_map/attend_forward/pallas_call | solution.py:195
  90.6 64.9 %middle_layer.1 = (bf16[1024,768]{1,0:T(8,128)(2,1)}, bf16[1024,768]{1,0:T(8,128)(2,1)}, bf16[1024,768]{1,0:T(8,128)(2,1)}, bf16[768,768]{1,0:T(8,128)(2,1)}, bf...) custom-call(bf16[1024,768]{1,0:T(8,128)(2,1)} %bitcast.67, ...), custom_call_target="tpu_custom_call" | custom-call | tf_op jit(solution)/shard_map/middle_layer/pallas_call | solution.py:838
  155.6 19.7 %attend_backward.2 = (bf16[2,512,768]{2,1,0:T(8,128)(2,1)}, bf16[2,512,768]{2,1,0:T(8,128)(2,1)}, bf16[2,512,768]{2,1,0:T(8,128)(2,1)}, bf16[2,512,768]{2,1,0:T(8,128)(2,1)}, bf16[2,512,768]{2,1,0:T(8,128)(2,1)}) custom-call(s32[2,2,3]{2,1,0:T(2,128)} %add_add_fusion.span_ref, bf16[2,512,768]{2,1,0:T(8,128)(2,1)} %bitcast.96, bf16[2,512,768]{2,1,0:T(8,128)(2,1)} %bitcast.99, ...), custom_call_target="tpu_custom_call" | custom-call | flops 20000000000 | bytes 20000000 | tf_op jit(solution)/shard_map/attend_backward/pallas_call | solution.py:223
  175.3 15.7 %attend_backward.3 = (bf16[2,512,768]{2,1,0:T(8,128)(2,1)}, bf16[2,512,768]{2,1,0:T(8,128)(2,1)}, bf16[2,512,768]{2,1,0:T(8,128)(2,1)}, bf16[2,512,768]{2,1,0:T(8,128)(2,1)}, bf16[2,512,768]{2,1,0:T(8,128)(2,1)}) custom-call(s32[2,2,3]{2,1,0:T(2,128)} %add_add_fusion.span_ref, ...), custom_call_target="tpu_custom_call", output_to_operand_aliasing={{0}: (12, {}), {1}: (13, {}), {2}: (14, {}), {3}: (15, {}),... | custom-call | flops 20000000000 | bytes 20000000 | tf_op jit(solution)/shard_map/attend_backward/pallas_call | solution.py:223
  191.0 73.7 %final_layer.1 = (bf16[4,192,768]{2,1,0:T(8,128)(2,1)}, bf16[192,3072]{1,0:T(8,128)(2,1)}, bf16[768,768]{1,0:T(8,128)(2,1)}, f32[16,768]{1,0:T(8,128)}, bf16[1024,768]{1,0:T(8,128)(2,1)}) custom-call(bf16[1024,768]{1,0:T(8,128)(2,1)} %bitcast.68, bf16[1024,768]{1,0:T(8,128)(2,1)} %bitcast.69, bf16[1024,768]{1,0:T(8,128)(2,1)} %bitcast.70, ...), custom_call_target="tpu_custom_call" | custom-call | tf_op jit(solution)/shard_map/final_layer/pallas_call | solution.py:1172
  264.8 1.5 convert_element_type.21
  266.2 1.4 slice_bitcast_fusion
  268.2 1.7 convert_element_type.22
  269.9 1.6 convert_element_type.23
  271.5 1.3 dynamic-slice_reduce_fusion
  272.8 1.7 fusion.18
  274.5 1.1 copy.110
  275.6 0.8 copy-done.7
  276.4 1.1 copy.111
  (52 shorter events, 4.6 us)
Async XLA Ops:
  0.7 3.2 %copy-start = (s32[2,1,12,16,3]{3,1,4,2,0:T(1,128)S(1)}, s32[2,1,12,16,3]{3,1,4,2,0:T(1,128)}, u32[]{:S(2)}) copy-start(s32[2,1,12,16,3]{3,1,4,2,0:T(1,128)} %param.21) | copy-start | bytes 13828
  1.6 7.1 %copy-start.1 = (bf16[768,768]{1,0:T(8,128)(2,1)S(1)}, bf16[768,768]{1,0:T(8,128)(2,1)}, u32[]{:S(2)}) copy-start(bf16[768,768]{1,0:T(8,128)(2,1)} %down_w_in.1) | copy-start | bytes 3538948
  1.6 7.1 %copy-start.3 = (bf16[192,3072]{1,0:T(8,128)(2,1)S(1)}, bf16[192,3072]{1,0:T(8,128)(2,1)}, u32[]{:S(2)}) copy-start(bf16[192,3072]{1,0:T(8,128)(2,1)} %up_in.1) | copy-start | bytes 3538948
  8.8 60.7 %copy-start.10 = (s32[2,1,1024]{2,1,0:T(1,128)S(1)}, s32[2,1,1024]{2,1,0:T(1,128)}, u32[]{:S(2)}) copy-start(s32[2,1,1024]{2,1,0:T(1,128)} %param.20) | copy-start | bytes 24580
  65.7 1.2 copy-start.2
  66.8 0.8 copy-start.4
  67.7 0.6 copy-start.5
  266.2 2.0 copy-start.9
  268.2 1.7 copy-start.8
  269.9 4.6 %copy-start.6 = (bf16[1024,768]{1,0:T(8,128)(2,1)S(1)}, bf16[1024,768]{1,0:T(8,128)(2,1)}, u32[]{:S(2)}) copy-start(bf16[1024,768]{1,0:T(8,128)(2,1)} %get-tuple-element.61) | copy-start | bytes 4718596
  274.5 2.0 copy-start.7
